TPU v7x, 128 devices: a whole 4x4x4 slice. The times are simulated.
128 devices in a mesh: gx: 4 (over z), gy: 16 (over y, x), gz: 2 (over core).
Axes of the slice: x: 4, y: 4, z: 4, core: 2. Of those that a mesh axis runs over, the one named last changes fastest.
Arguments:
- particles: float32 [8, 1048576], P(None, ('gx', 'gy', 'gz')), may hold values from -0.5 to 0.5
- dest_key: int32 [1048576], P(('gx', 'gy', 'gz')), may hold values from 0 to 127, as said below
- cell_a: int32 [1048576], P(('gx', 'gy', 'gz')), may hold values from 0 to 255
- cell_b: int32 [1048576], P(('gx', 'gy', 'gz')), may hold values from 0 to 127
- velocity: float32 [2, 1024, 4096], P(None, 'gx', ('gy', 'gz')), may hold values from -6 to 6
Outputs:
- binned: float32 [8, 4194304], P(None, ('gx', 'gy', 'gz'))
- binned_cell: int32 [4194304], P(('gx', 'gy', 'gz'))
Inputs may be any that keep to these rules, and one draw needn't show every extreme that they name: Of the particles of one device at most 256 have any one value of dest_key, and one device is named by exactly 256 particles of every device.
All inputs are finite; a program needn't handle non-finite values.
Results may differ from a plain program's by a relative error of at most 0.0003.
Values sent between devices are 32-bit elements; how exact they have to be, the bound alone decides.
A program may use at most 64 MiB of HBM per device.

v0:
```python
import math

import jax
import jax.numpy as jnp
from jax import lax
from jax.sharding import Mesh
from jax.sharding import PartitionSpec as P

GX_GY_GZ = ("gx", "gy_0", "gy_1", "gz")
GY_GZ = ("gy_0", "gy_1", "gz")


step_length = 0.5


def extended(x, sides, width):
    for axis, dim in sides:
        peers, length = (lax.axis_size(axis), x.shape[dim])
        up = [(i, (i + 1) % peers) for i in range(peers - 1)]
        down = [(j, i) for i, j in up]
        last = lax.slice_in_dim(x, length - width, length, axis=dim)
        initial = lax.slice_in_dim(x, 0, width, axis=dim)
        before = lax.ppermute(last, axis, up)
        after = lax.ppermute(initial, axis, down)
        x = jnp.concatenate([before, x, after], axis=dim)
    return x


def split_up(x, dim, peers):
    before, after = (x.shape[:dim], x.shape[dim + 1 :])
    return jnp.moveaxis(x.reshape(*before, peers, -1, *after), dim, 0)


def in_order(pieces, dim):
    pieces = jnp.moveaxis(pieces, 0, dim)
    lengths = pieces.shape
    return pieces.reshape(*lengths[:dim], lengths[dim] * lengths[dim + 1], *lengths[dim + 2 :])


def turned_blocks(pieces, axes, sequence):
    lengths = [lax.axis_size(a) for a in axes]
    pieces = pieces.reshape(*lengths, *pieces.shape[1:])
    for k in sequence:
        pieces = lax.all_to_all(pieces, axes[k], split_axis=k, concat_axis=k, tiled=True)
    return pieces.reshape(-1, *pieces.shape[len(axes) :])


def core_and_chips(x, groups, sequence, split_dim, concat_dim):
    peers = lax.axis_size(groups[0]) * lax.axis_size(groups[1])
    pieces = split_up(x, split_dim, peers)
    return in_order(turned_blocks(pieces, groups, sequence), concat_dim)


def quad_weights(frac):
    return (0.5 * frac * (frac - 1.0), 1.0 - frac * frac, 0.5 * frac * (frac + 1.0))


def counted_ranks(dest_key, owners):
    block_size = math.gcd(dest_key.shape[0], 1024)
    owner_ids = lax.iota(jnp.int32, owners)
    lower = (
        lax.iota(jnp.int32, block_size)[:, None] > lax.iota(jnp.int32, block_size)[None, :]
    ).astype(jnp.bfloat16)

    def rank_block(seen_counts, keys_block):
        one_hot = (keys_block[:, None] == owner_ids[None, :]).astype(jnp.float32)
        before = jnp.dot(lower, one_hot.astype(jnp.bfloat16), preferred_element_type=jnp.float32)
        block_ranks = jnp.sum((before + seen_counts[None, :]) * one_hot, axis=1)
        return (seen_counts + jnp.sum(one_hot, axis=0), block_ranks.astype(jnp.int32))

    start_counts = jnp.zeros((owners,), jnp.float32)
    unused, ranks = lax.scan(rank_block, start_counts, dest_key.reshape(-1, block_size))
    return ranks.reshape(-1)


def bucket_rows(payload, dest_key, ranking, owners, capacity):
    count = dest_key.shape[0]
    block_size = math.gcd(count, 1024)
    owner_ids = lax.iota(jnp.int32, owners)
    rank_ids = lax.iota(jnp.int32, capacity)
    rows = payload.shape[0]

    def add_block(total, index):
        start = index * block_size
        keys_block = lax.dynamic_slice_in_dim(dest_key, start, block_size, 0)
        ranks_block = lax.dynamic_slice_in_dim(ranking, start, block_size, 0)
        values = lax.dynamic_slice_in_dim(payload, start, block_size, 1)
        owner_hot = (keys_block[:, None] == owner_ids[None, :]).astype(jnp.float32)
        rank_hot = (ranks_block[:, None] == rank_ids[None, :]).astype(jnp.float32)
        spread = values[:, :, None] * rank_hot[None, :, :]
        placed = lax.dot_general(
            spread,
            owner_hot,
            (((1,), (0,)), ((), ())),
            precision=lax.Precision.HIGHEST,
            preferred_element_type=jnp.float32,
        )
        return (total + placed, None)

    start_total = jnp.zeros((rows, capacity, owners), jnp.float32)
    total, unused = lax.scan(
        add_block, start_total, jnp.arange(count // block_size, dtype=jnp.int32)
    )
    return jnp.transpose(total, (0, 2, 1))


def shards(particles, dest_key, cell_a, cell_b, velocity):
    owners = lax.axis_size(GX_GY_GZ)
    particle_count = particles.shape[1]
    capacity = 4 * particle_count // owners
    tile_height = velocity.shape[1]
    tile_width = velocity.shape[2]
    ranking = counted_ranks(dest_key, owners)
    cell_shifted = (cell_a * tile_width + cell_b + 1).astype(jnp.float32)
    payload = jnp.concatenate([particles, cell_shifted[None, :]], axis=0)
    placed = bucket_rows(payload, dest_key, ranking, owners, capacity)
    outgoing = jnp.concatenate([placed[0:8], placed[8:9] - 1.0], axis=0)
    padded = extended(velocity, (("gx", 1), (GY_GZ, 2)), 1)
    padded_width = tile_width + 2
    both_fields = jnp.concatenate([padded[0], padded[1]], axis=1)
    row_ids = lax.iota(jnp.int32, tile_height + 2)
    col_ids = lax.iota(jnp.int32, padded_width)

    def interpolate(arrived_block):
        cell_ids = arrived_block[8].astype(jnp.int32)
        is_live = cell_ids >= 0
        safe_ids = jnp.maximum(cell_ids, 0)
        node_row = safe_ids // tile_width
        node_col = safe_ids % tile_width
        weights_a = quad_weights(arrived_block[0])
        weights_b = quad_weights(arrived_block[1])
        row_weight = jnp.zeros((cell_ids.shape[0], tile_height + 2), jnp.float32)
        col_weight = jnp.zeros((cell_ids.shape[0], padded_width), jnp.float32)
        for shift in range(3):
            row_weight = row_weight + weights_a[shift][:, None] * (
                node_row[:, None] + shift == row_ids[None, :]
            ).astype(jnp.float32)
            col_weight = col_weight + weights_b[shift][:, None] * (
                node_col[:, None] + shift == col_ids[None, :]
            ).astype(jnp.float32)
        rows_mixed = jnp.dot(
            row_weight,
            both_fields,
            precision=lax.Precision.HIGHEST,
            preferred_element_type=jnp.float32,
        )
        speed_first = jnp.sum(rows_mixed[:, :padded_width] * col_weight, axis=1)
        speed_second = jnp.sum(rows_mixed[:, padded_width:] * col_weight, axis=1)
        speed = jnp.stack([speed_first, speed_second], axis=0)
        return jnp.where(is_live[None], step_length * speed, 0.0)

    arrived = core_and_chips(outgoing, (("gx", "gy_0", "gy_1"), "gz"), (1, 0), 1, 1)
    flat = arrived.reshape(9, -1)
    count = flat.shape[1]
    block_size = math.gcd(count, 2048)

    def one_block(index):
        return interpolate(lax.dynamic_slice_in_dim(flat, index * block_size, block_size, 1))

    displace = lax.map(one_block, jnp.arange(count // block_size, dtype=jnp.int32))
    displace = jnp.transpose(displace, (1, 0, 2)).reshape(2, count)
    advanced = jnp.concatenate([flat[0:2], flat[2:4] + displace, flat[4:8]], axis=0)
    cell_ids = flat[8].astype(jnp.int32)
    advanced, cell_rows = (
        advanced.reshape((8,) + arrived.shape[1:]),
        cell_ids.reshape((1,) + arrived.shape[1:]),
    )
    binned = advanced.reshape(8, -1)
    binned_cell = cell_rows.reshape(-1)
    return (binned, binned_cell)


def solution(mesh):
    split = Mesh(
        mesh.devices.reshape(mesh.shape["gx"], 4, 4, mesh.shape["gz"]), ("gx", "gy_0", "gy_1", "gz")
    )
    in_specs = (P(None, GX_GY_GZ), P(GX_GY_GZ), P(GX_GY_GZ), P(GX_GY_GZ), P(None, "gx", GY_GZ))
    out_specs = (P(None, GX_GY_GZ), P(GX_GY_GZ))
    return jax.shard_map(
        shards, mesh=split, in_specs=in_specs, out_specs=out_specs, check_vma=False
    )
```

profile of v0, /device:TPU:43, one launch (start us, length us, event | category | flops | bytes accessed | tf_op | source)
XLA Modules:
  0.0 259.1 jit_solution(3912188636909918199)
XLA Ops:
  0.7 0.8 reshape.317
  1.5 7.5 %while.40 = (s32[]{:T(128)}, f32[128]{0:T(128)S(1)}, s32[8,1024]{1,0:T(8,128)S(1)}, s32[8,1024]{1,0:T(8,128)S(1)}, s32[]{:T(128)}, /*index=5*/s32[]{:T(128)}) while((s32[]{:T(128)}, f32[128]{0:T(128)S(1)}, s32[8,1024]{1,0:T(8,128)S(1)}, s32[8,1024]{1,0:T(8,128)S(1)}, s32[]{:T(128)}, /*index=5*/s32[]{:T(128)}) %tuple.104), condition=%wide.region_3.4_spmd.clone, body=%wide.region_0.3_spmd.clone.sunk | while | flops 271843456 | bytes 40023 | solution.py:72
  9.1 59.6 %while.41 = (s32[]{:T(128)}, f32[9,256,128]{2,1,0:T(8,128)S(1)}, s32[8]{0:T(128)S(1)}, f32[9,8192]{1,0:T(8,128)S(1)}, s32[8192]{0:T(1024)S(1)}, /*index=5*/s32[8...) while((s32[]{:T(128)}, f32[9,256,128]{2,1,0:T(8,128)S(1)}, s32[8]{0:T(128)S(1)}, ...), condition=%wide.region_5.6_spmd.clone, body=%wide.region_4.5_spmd.clone.sunk | while | flops 3627483136 | bytes 4591797 | solution.py:101
  10.6 0.7 dynamic_slice.54
  11.3 5.3 %fusion.85 = f32[9,256,128]{2,1,0:T(8,128)S(1)} fusion(f32[1024,256]{0,1:T(8,128)S(1)} %fusion.84, f32[9,1024]{1,0:T(8,128)S(1)} %constant_dynamic-slice_fusion.6, f32[9,256,128]{2,1,0:T(8,128)S(1)} %get-tuple-element.513, pred[]{:T(512)S(6)} %compare.16, s32[1024]{0:T(1024)S(1)} %dynamic_slice.54), kind=kOutput, calls=%fused_computation.23.clone.1 | convolution fusion | flops 3626958848 | bytes 3448833 | tf_op jit(solution)/shard_map/while/body/eval_jaxpr/dot_general | solution.py:91
  18.0 0.7 dynamic_slice.54
  18.7 5.3 %fusion.85 = f32[9,256,128]{2,1,0:T(8,128)S(1)} fusion(f32[1024,256]{0,1:T(8,128)S(1)} %fusion.84, f32[9,1024]{1,0:T(8,128)S(1)} %constant_dynamic-slice_fusion.6, f32[9,256,128]{2,1,0:T(8,128)S(1)} %get-tuple-element.513, pred[]{:T(512)S(6)} %compare.16, s32[1024]{0:T(1024)S(1)} %dynamic_slice.54), kind=kOutput, calls=%fused_computation.23.clone.1 | convolution fusion | flops 3626958848 | bytes 3448833 | tf_op jit(solution)/shard_map/while/body/eval_jaxpr/dot_general | solution.py:91
  25.5 0.7 dynamic_slice.54
  26.2 5.3 %fusion.85 = f32[9,256,128]{2,1,0:T(8,128)S(1)} fusion(f32[1024,256]{0,1:T(8,128)S(1)} %fusion.84, f32[9,1024]{1,0:T(8,128)S(1)} %constant_dynamic-slice_fusion.6, f32[9,256,128]{2,1,0:T(8,128)S(1)} %get-tuple-element.513, pred[]{:T(512)S(6)} %compare.16, s32[1024]{0:T(1024)S(1)} %dynamic_slice.54), kind=kOutput, calls=%fused_computation.23.clone.1 | convolution fusion | flops 3626958848 | bytes 3448833 | tf_op jit(solution)/shard_map/while/body/eval_jaxpr/dot_general | solution.py:91
  32.9 0.7 dynamic_slice.54
  33.6 5.3 %fusion.85 = f32[9,256,128]{2,1,0:T(8,128)S(1)} fusion(f32[1024,256]{0,1:T(8,128)S(1)} %fusion.84, f32[9,1024]{1,0:T(8,128)S(1)} %constant_dynamic-slice_fusion.6, f32[9,256,128]{2,1,0:T(8,128)S(1)} %get-tuple-element.513, pred[]{:T(512)S(6)} %compare.16, s32[1024]{0:T(1024)S(1)} %dynamic_slice.54), kind=kOutput, calls=%fused_computation.23.clone.1 | convolution fusion | flops 3626958848 | bytes 3448833 | tf_op jit(solution)/shard_map/while/body/eval_jaxpr/dot_general | solution.py:91
  40.4 0.7 dynamic_slice.54
  41.1 5.3 %fusion.85 = f32[9,256,128]{2,1,0:T(8,128)S(1)} fusion(f32[1024,256]{0,1:T(8,128)S(1)} %fusion.84, f32[9,1024]{1,0:T(8,128)S(1)} %constant_dynamic-slice_fusion.6, f32[9,256,128]{2,1,0:T(8,128)S(1)} %get-tuple-element.513, pred[]{:T(512)S(6)} %compare.16, s32[1024]{0:T(1024)S(1)} %dynamic_slice.54), kind=kOutput, calls=%fused_computation.23.clone.1 | convolution fusion | flops 3626958848 | bytes 3448833 | tf_op jit(solution)/shard_map/while/body/eval_jaxpr/dot_general | solution.py:91
  47.8 0.7 dynamic_slice.54
  48.5 5.3 %fusion.85 = f32[9,256,128]{2,1,0:T(8,128)S(1)} fusion(f32[1024,256]{0,1:T(8,128)S(1)} %fusion.84, f32[9,1024]{1,0:T(8,128)S(1)} %constant_dynamic-slice_fusion.6, f32[9,256,128]{2,1,0:T(8,128)S(1)} %get-tuple-element.513, pred[]{:T(512)S(6)} %compare.16, s32[1024]{0:T(1024)S(1)} %dynamic_slice.54), kind=kOutput, calls=%fused_computation.23.clone.1 | convolution fusion | flops 3626958848 | bytes 3448833 | tf_op jit(solution)/shard_map/while/body/eval_jaxpr/dot_general | solution.py:91
  55.3 0.7 dynamic_slice.54
  56.0 5.3 %fusion.85 = f32[9,256,128]{2,1,0:T(8,128)S(1)} fusion(f32[1024,256]{0,1:T(8,128)S(1)} %fusion.84, f32[9,1024]{1,0:T(8,128)S(1)} %constant_dynamic-slice_fusion.6, f32[9,256,128]{2,1,0:T(8,128)S(1)} %get-tuple-element.513, pred[]{:T(512)S(6)} %compare.16, s32[1024]{0:T(1024)S(1)} %dynamic_slice.54), kind=kOutput, calls=%fused_computation.23.clone.1 | convolution fusion | flops 3626958848 | bytes 3448833 | tf_op jit(solution)/shard_map/while/body/eval_jaxpr/dot_general | solution.py:91
  62.7 0.7 dynamic_slice.54
  63.4 5.3 %fusion.85 = f32[9,256,128]{2,1,0:T(8,128)S(1)} fusion(f32[1024,256]{0,1:T(8,128)S(1)} %fusion.84, f32[9,1024]{1,0:T(8,128)S(1)} %constant_dynamic-slice_fusion.6, f32[9,256,128]{2,1,0:T(8,128)S(1)} %get-tuple-element.513, pred[]{:T(512)S(6)} %compare.16, s32[1024]{0:T(1024)S(1)} %dynamic_slice.54), kind=kOutput, calls=%fused_computation.23.clone.1 | convolution fusion | flops 3626958848 | bytes 3448833 | tf_op jit(solution)/shard_map/while/body/eval_jaxpr/dot_general | solution.py:91
  69.0 1.8 copy.25
  70.8 0.8 copy.26
  71.6 5.0 %all_to_all.10 = f32[64,2,9,1,256]{4,3,2,0,1:T(1,128)S(1)} all-to-all(f32[64,2,9,1,256]{4,3,2,0,1:T(1,128)S(1)} %copy.26), channel_id=1, replica_groups=mesh['gx'=4,'gy_0'=4,'gy_1'=4,'gz'=2] {'gz'}, dimensions={1} | all-to-all | bytes 2359296 | tf_op jit(solution)/shard_map/all_to_all | solution.py:44
  76.6 1.8 copy.27
  78.4 10.5 %all-to-all-start.1 = ((f32[64,2,9,1,256]{4,3,2,1,0:T(1,128)}), f32[64,2,9,1,256]{4,3,2,1,0:T(1,128)S(1)}, u32[]{:S(2)}, u32[]{:S(2)}) async-start(f32[64,2,9,1,256]{4,3,2,1,0:T(1,128)} %copy.27), calls=%async_computation.1 | async-start | bytes 2359296 | tf_op jit(solution)/shard_map/all_to_all | solution.py:44
  88.9 3.2 %collective-permute-start = (f32[2,1,128]{2,1,0:T(1,128)S(1)}, f32[2,1,128]{2,1,0:T(1,128)S(1)}, u32[]{:S(2)}, u32[]{:S(2)}) collective-permute-start(f32[2,1,128]{2,1,0:T(1,128)S(1)} %get-tuple-element.349), channel_id=1, source_target_pairs={{0,32},{32,64},{64,96},{1,33},{33,65},{65,97},{2,34},{34,66},{66,9... | collective-permute-start | bytes 3080 | tf_op jit(solution)/shard_map/ppermute | solution.py:23
  92.2 2.1 collective-permute-start.1
  94.2 1.8 collective-permute-done
  96.0 1.5 collective-permute-done.1
  97.7 10.0 %collective-permute-start.2 = (f32[2,258,1]{2,1,0:T(8,128)S(1)}, f32[2,258,1]{2,1,0:T(8,128)S(1)}, u32[]{:S(2)}, u32[]{:S(2)}) collective-permute-start(f32[2,258,1]{2,1,0:T(8,128)S(1)} %get-tuple-element.347), channel_id=1, source_target_pairs={{0,1},{1,2},{2,3},{3,4},{4,5},{5,6},{6,7},{7,8},{8,9},{9,10},{10,1... | collective-permute-start | bytes 6200 | tf_op jit(solution)/shard_map/ppermute | solution.py:23
  107.7 2.1 collective-permute-start.3
  109.8 1.3 collective-permute-done.2
  111.1 4.4 %collective-permute-done.3 = f32[2,258,1]{2,1,0:T(8,128)S(1)} collective-permute-done((f32[2,258,1]{2,1,0:T(8,128)S(1)}, f32[2,258,1]{2,1,0:T(8,128)S(1)}, u32[]{:S(2)}, u32[]{:S(2)}) %collective-permute-start.3) | collective-permute-done | bytes 2096 | tf_op jit(solution)/shard_map/ppermute | solution.py:24
  115.8 0.9 pad_maximum_fusion.3
  117.6 0.7 slice_convert_fusion
  118.5 1.2 copy.35
  119.7 137.0 %while.39 = (s32[]{:T(128)}, f32[16,2,2048]{2,1,0:T(2,128)S(1)}, s32[16]{0:T(128)S(1)}, f32[9,32768]{1,0:T(8,128)S(1)}, f32[258,260]{1,0:T(8,128)}, /*index=5*/s...) while((s32[]{:T(128)}, f32[16,2,2048]{2,1,0:T(2,128)S(1)}, ...), condition=%wide.region_9.10_spmd.clone.clone, body=%wide.region_6.9_spmd.clone.clone.sunk | while | flops 1656059904 | bytes 4856059 | solution.py:160
  121.4 6.3 %fusion.76 = f32[2048,260]{0,1:T(8,128)S(1)} fusion(f32[258,260]{1,0:T(8,128)} %get-tuple-element.558, f32[2048]{0:T(1024)S(1)} %bitcast.130, s32[2048]{0:T(1024)S(1)} %broadcast_add_fusion.5, f32[2048]{0:T(1024)S(1)} %bitcast.129, s32[2048]{0:T(1024)S(1)} %get-tuple-element.461, f32[2048]{0:T(1024)S(1)} %bitcast.128, s32[2048]{0:T(1024)S(1)} %get-tuple-element.459), kind=kOutput, calls=%fused_computation.33.clone.1 | convolution fusion | flops 1652785152 | bytes 2447392 | tf_op jit(solution)/shard_map/while/body/eval_jaxpr/dot_general | solution.py:141
  128.3 0.7 dynamic_slice.49
  129.9 6.3 %fusion.76 = f32[2048,260]{0,1:T(8,128)S(1)} fusion(f32[258,260]{1,0:T(8,128)} %get-tuple-element.558, f32[2048]{0:T(1024)S(1)} %bitcast.130, s32[2048]{0:T(1024)S(1)} %broadcast_add_fusion.5, f32[2048]{0:T(1024)S(1)} %bitcast.129, s32[2048]{0:T(1024)S(1)} %get-tuple-element.461, f32[2048]{0:T(1024)S(1)} %bitcast.128, s32[2048]{0:T(1024)S(1)} %get-tuple-element.459), kind=kOutput, calls=%fused_computation.33.clone.1 | convolution fusion | flops 1652785152 | bytes 2447392 | tf_op jit(solution)/shard_map/while/body/eval_jaxpr/dot_general | solution.py:141
  136.9 0.7 dynamic_slice.49
  138.5 6.3 %fusion.76 = f32[2048,260]{0,1:T(8,128)S(1)} fusion(f32[258,260]{1,0:T(8,128)} %get-tuple-element.558, f32[2048]{0:T(1024)S(1)} %bitcast.130, s32[2048]{0:T(1024)S(1)} %broadcast_add_fusion.5, f32[2048]{0:T(1024)S(1)} %bitcast.129, s32[2048]{0:T(1024)S(1)} %get-tuple-element.461, f32[2048]{0:T(1024)S(1)} %bitcast.128, s32[2048]{0:T(1024)S(1)} %get-tuple-element.459), kind=kOutput, calls=%fused_computation.33.clone.1 | convolution fusion | flops 1652785152 | bytes 2447392 | tf_op jit(solution)/shard_map/while/body/eval_jaxpr/dot_general | solution.py:141
  145.4 0.7 dynamic_slice.49
  147.1 6.3 %fusion.76 = f32[2048,260]{0,1:T(8,128)S(1)} fusion(f32[258,260]{1,0:T(8,128)} %get-tuple-element.558, f32[2048]{0:T(1024)S(1)} %bitcast.130, s32[2048]{0:T(1024)S(1)} %broadcast_add_fusion.5, f32[2048]{0:T(1024)S(1)} %bitcast.129, s32[2048]{0:T(1024)S(1)} %get-tuple-element.461, f32[2048]{0:T(1024)S(1)} %bitcast.128, s32[2048]{0:T(1024)S(1)} %get-tuple-element.459), kind=kOutput, calls=%fused_computation.33.clone.1 | convolution fusion | flops 1652785152 | bytes 2447392 | tf_op jit(solution)/shard_map/while/body/eval_jaxpr/dot_general | solution.py:141
  154.0 0.7 dynamic_slice.49
  155.6 6.3 %fusion.76 = f32[2048,260]{0,1:T(8,128)S(1)} fusion(f32[258,260]{1,0:T(8,128)} %get-tuple-element.558, f32[2048]{0:T(1024)S(1)} %bitcast.130, s32[2048]{0:T(1024)S(1)} %broadcast_add_fusion.5, f32[2048]{0:T(1024)S(1)} %bitcast.129, s32[2048]{0:T(1024)S(1)} %get-tuple-element.461, f32[2048]{0:T(1024)S(1)} %bitcast.128, s32[2048]{0:T(1024)S(1)} %get-tuple-element.459), kind=kOutput, calls=%fused_computation.33.clone.1 | convolution fusion | flops 1652785152 | bytes 2447392 | tf_op jit(solution)/shard_map/while/body/eval_jaxpr/dot_general | solution.py:141
  162.6 0.7 dynamic_slice.49
  164.2 6.3 %fusion.76 = f32[2048,260]{0,1:T(8,128)S(1)} fusion(f32[258,260]{1,0:T(8,128)} %get-tuple-element.558, f32[2048]{0:T(1024)S(1)} %bitcast.130, s32[2048]{0:T(1024)S(1)} %broadcast_add_fusion.5, f32[2048]{0:T(1024)S(1)} %bitcast.129, s32[2048]{0:T(1024)S(1)} %get-tuple-element.461, f32[2048]{0:T(1024)S(1)} %bitcast.128, s32[2048]{0:T(1024)S(1)} %get-tuple-element.459), kind=kOutput, calls=%fused_computation.33.clone.1 | convolution fusion | flops 1652785152 | bytes 2447392 | tf_op jit(solution)/shard_map/while/body/eval_jaxpr/dot_general | solution.py:141
  172.7 6.3 %fusion.76 = f32[2048,260]{0,1:T(8,128)S(1)} fusion(f32[258,260]{1,0:T(8,128)} %get-tuple-element.558, f32[2048]{0:T(1024)S(1)} %bitcast.130, s32[2048]{0:T(1024)S(1)} %broadcast_add_fusion.5, f32[2048]{0:T(1024)S(1)} %bitcast.129, s32[2048]{0:T(1024)S(1)} %get-tuple-element.461, f32[2048]{0:T(1024)S(1)} %bitcast.128, s32[2048]{0:T(1024)S(1)} %get-tuple-element.459), kind=kOutput, calls=%fused_computation.33.clone.1 | convolution fusion | flops 1652785152 | bytes 2447392 | tf_op jit(solution)/shard_map/while/body/eval_jaxpr/dot_general | solution.py:141
  179.7 0.7 dynamic_slice.49
  181.3 6.3 %fusion.76 = f32[2048,260]{0,1:T(8,128)S(1)} fusion(f32[258,260]{1,0:T(8,128)} %get-tuple-element.558, f32[2048]{0:T(1024)S(1)} %bitcast.130, s32[2048]{0:T(1024)S(1)} %broadcast_add_fusion.5, f32[2048]{0:T(1024)S(1)} %bitcast.129, s32[2048]{0:T(1024)S(1)} %get-tuple-element.461, f32[2048]{0:T(1024)S(1)} %bitcast.128, s32[2048]{0:T(1024)S(1)} %get-tuple-element.459), kind=kOutput, calls=%fused_computation.33.clone.1 | convolution fusion | flops 1652785152 | bytes 2447392 | tf_op jit(solution)/shard_map/while/body/eval_jaxpr/dot_general | solution.py:141
  188.2 0.7 dynamic_slice.49
  189.9 6.3 %fusion.76 = f32[2048,260]{0,1:T(8,128)S(1)} fusion(f32[258,260]{1,0:T(8,128)} %get-tuple-element.558, f32[2048]{0:T(1024)S(1)} %bitcast.130, s32[2048]{0:T(1024)S(1)} %broadcast_add_fusion.5, f32[2048]{0:T(1024)S(1)} %bitcast.129, s32[2048]{0:T(1024)S(1)} %get-tuple-element.461, f32[2048]{0:T(1024)S(1)} %bitcast.128, s32[2048]{0:T(1024)S(1)} %get-tuple-element.459), kind=kOutput, calls=%fused_computation.33.clone.1 | convolution fusion | flops 1652785152 | bytes 2447392 | tf_op jit(solution)/shard_map/while/body/eval_jaxpr/dot_general | solution.py:141
  196.8 0.7 dynamic_slice.49
  198.4 6.3 %fusion.76 = f32[2048,260]{0,1:T(8,128)S(1)} fusion(f32[258,260]{1,0:T(8,128)} %get-tuple-element.558, f32[2048]{0:T(1024)S(1)} %bitcast.130, s32[2048]{0:T(1024)S(1)} %broadcast_add_fusion.5, f32[2048]{0:T(1024)S(1)} %bitcast.129, s32[2048]{0:T(1024)S(1)} %get-tuple-element.461, f32[2048]{0:T(1024)S(1)} %bitcast.128, s32[2048]{0:T(1024)S(1)} %get-tuple-element.459), kind=kOutput, calls=%fused_computation.33.clone.1 | convolution fusion | flops 1652785152 | bytes 2447392 | tf_op jit(solution)/shard_map/while/body/eval_jaxpr/dot_general | solution.py:141
  205.4 0.7 dynamic_slice.49
  207.0 6.3 %fusion.76 = f32[2048,260]{0,1:T(8,128)S(1)} fusion(f32[258,260]{1,0:T(8,128)} %get-tuple-element.558, f32[2048]{0:T(1024)S(1)} %bitcast.130, s32[2048]{0:T(1024)S(1)} %broadcast_add_fusion.5, f32[2048]{0:T(1024)S(1)} %bitcast.129, s32[2048]{0:T(1024)S(1)} %get-tuple-element.461, f32[2048]{0:T(1024)S(1)} %bitcast.128, s32[2048]{0:T(1024)S(1)} %get-tuple-element.459), kind=kOutput, calls=%fused_computation.33.clone.1 | convolution fusion | flops 1652785152 | bytes 2447392 | tf_op jit(solution)/shard_map/while/body/eval_jaxpr/dot_general | solution.py:141
  213.9 0.7 dynamic_slice.49
  215.5 6.3 %fusion.76 = f32[2048,260]{0,1:T(8,128)S(1)} fusion(f32[258,260]{1,0:T(8,128)} %get-tuple-element.558, f32[2048]{0:T(1024)S(1)} %bitcast.130, s32[2048]{0:T(1024)S(1)} %broadcast_add_fusion.5, f32[2048]{0:T(1024)S(1)} %bitcast.129, s32[2048]{0:T(1024)S(1)} %get-tuple-element.461, f32[2048]{0:T(1024)S(1)} %bitcast.128, s32[2048]{0:T(1024)S(1)} %get-tuple-element.459), kind=kOutput, calls=%fused_computation.33.clone.1 | convolution fusion | flops 1652785152 | bytes 2447392 | tf_op jit(solution)/shard_map/while/body/eval_jaxpr/dot_general | solution.py:141
  224.1 6.3 %fusion.76 = f32[2048,260]{0,1:T(8,128)S(1)} fusion(f32[258,260]{1,0:T(8,128)} %get-tuple-element.558, f32[2048]{0:T(1024)S(1)} %bitcast.130, s32[2048]{0:T(1024)S(1)} %broadcast_add_fusion.5, f32[2048]{0:T(1024)S(1)} %bitcast.129, s32[2048]{0:T(1024)S(1)} %get-tuple-element.461, f32[2048]{0:T(1024)S(1)} %bitcast.128, s32[2048]{0:T(1024)S(1)} %get-tuple-element.459), kind=kOutput, calls=%fused_computation.33.clone.1 | convolution fusion | flops 1652785152 | bytes 2447392 | tf_op jit(solution)/shard_map/while/body/eval_jaxpr/dot_general | solution.py:141
  231.0 0.7 dynamic_slice.49
  232.7 6.3 %fusion.76 = f32[2048,260]{0,1:T(8,128)S(1)} fusion(f32[258,260]{1,0:T(8,128)} %get-tuple-element.558, f32[2048]{0:T(1024)S(1)} %bitcast.130, s32[2048]{0:T(1024)S(1)} %broadcast_add_fusion.5, f32[2048]{0:T(1024)S(1)} %bitcast.129, s32[2048]{0:T(1024)S(1)} %get-tuple-element.461, f32[2048]{0:T(1024)S(1)} %bitcast.128, s32[2048]{0:T(1024)S(1)} %get-tuple-element.459), kind=kOutput, calls=%fused_computation.33.clone.1 | convolution fusion | flops 1652785152 | bytes 2447392 | tf_op jit(solution)/shard_map/while/body/eval_jaxpr/dot_general | solution.py:141
  241.2 6.3 %fusion.76 = f32[2048,260]{0,1:T(8,128)S(1)} fusion(f32[258,260]{1,0:T(8,128)} %get-tuple-element.558, f32[2048]{0:T(1024)S(1)} %bitcast.130, s32[2048]{0:T(1024)S(1)} %broadcast_add_fusion.5, f32[2048]{0:T(1024)S(1)} %bitcast.129, s32[2048]{0:T(1024)S(1)} %get-tuple-element.461, f32[2048]{0:T(1024)S(1)} %bitcast.128, s32[2048]{0:T(1024)S(1)} %get-tuple-element.459), kind=kOutput, calls=%fused_computation.33.clone.1 | convolution fusion | flops 1652785152 | bytes 2447392 | tf_op jit(solution)/shard_map/while/body/eval_jaxpr/dot_general | solution.py:141
  249.8 6.3 %fusion.76 = f32[2048,260]{0,1:T(8,128)S(1)} fusion(f32[258,260]{1,0:T(8,128)} %get-tuple-element.558, f32[2048]{0:T(1024)S(1)} %bitcast.130, s32[2048]{0:T(1024)S(1)} %broadcast_add_fusion.5, f32[2048]{0:T(1024)S(1)} %bitcast.129, s32[2048]{0:T(1024)S(1)} %get-tuple-element.461, f32[2048]{0:T(1024)S(1)} %bitcast.128, s32[2048]{0:T(1024)S(1)} %get-tuple-element.459), kind=kOutput, calls=%fused_computation.33.clone.1 | convolution fusion | flops 1652785152 | bytes 2447392 | tf_op jit(solution)/shard_map/while/body/eval_jaxpr/dot_general | solution.py:141
  257.8 1.3 pad_maximum_fusion
  (233 shorter events, 32.1 us)
Async XLA Ops:
  1.4 7.6 %copy-start.2 = (s32[8192]{0:T(1024)S(1)}, s32[8192]{0:T(1024)}, u32[]{:S(2)}) copy-start(s32[8192]{0:T(1024)} %param.14) | copy-start | bytes 98308
  1.4 7.6 %copy-start.3 = (s32[8192]{0:T(1024)S(1)}, s32[8192]{0:T(1024)}, u32[]{:S(2)}) copy-start(s32[8192]{0:T(1024)} %param.13) | copy-start | bytes 98308
  1.5 7.6 %copy-start.1 = (f32[8,8192]{1,0:T(8,128)S(1)}, f32[8,8192]{1,0:T(8,128)}, u32[]{:S(2)}) copy-start(f32[8,8192]{1,0:T(8,128)} %param.11) | copy-start | bytes 786436
  78.4 10.5 %copy-start = (f32[2,256,128]{2,1,0:T(8,128)S(1)}, f32[2,256,128]{2,1,0:T(8,128)}, u32[]{:S(2)}) copy-start(f32[2,256,128]{2,1,0:T(8,128)} %param.15) | copy-start | bytes 786436
  78.4 38.3 %all-to-all-start.1 = ((f32[64,2,9,1,256]{4,3,2,1,0:T(1,128)}), f32[64,2,9,1,256]{4,3,2,1,0:T(1,128)S(1)}, u32[]{:S(2)}, u32[]{:S(2)}) async-start(f32[64,2,9,1,256]{4,3,2,1,0:T(1,128)} %copy.27), calls=%async_computation.1 | async-start | bytes 2359296 | tf_op jit(solution)/shard_map/all_to_all | solution.py:44
  88.9 7.1 %collective-permute-start = (f32[2,1,128]{2,1,0:T(1,128)S(1)}, f32[2,1,128]{2,1,0:T(1,128)S(1)}, u32[]{:S(2)}, u32[]{:S(2)}) collective-permute-start(f32[2,1,128]{2,1,0:T(1,128)S(1)} %get-tuple-element.349), channel_id=1, source_target_pairs={{0,32},{32,64},{64,96},{1,33},{33,65},{65,97},{2,34},{34,66},{66,9... | collective-permute-start | bytes 3080 | tf_op jit(solution)/shard_map/ppermute | solution.py:23
  92.2 5.4 %collective-permute-start.1 = (f32[2,1,128]{2,1,0:T(1,128)S(1)}, f32[2,1,128]{2,1,0:T(1,128)S(1)}, u32[]{:S(2)}, u32[]{:S(2)}) collective-permute-start(f32[2,1,128]{2,1,0:T(1,128)S(1)} %get-tuple-element.350), channel_id=1, source_target_pairs={{32,0},{64,32},{96,64},{33,1},{65,33},{97,65},{34,2},{66,34},{98,6... | collective-permute-start | bytes 3080 | tf_op jit(solution)/shard_map/ppermute | solution.py:24
  97.7 13.4 %collective-permute-start.2 = (f32[2,258,1]{2,1,0:T(8,128)S(1)}, f32[2,258,1]{2,1,0:T(8,128)S(1)}, u32[]{:S(2)}, u32[]{:S(2)}) collective-permute-start(f32[2,258,1]{2,1,0:T(8,128)S(1)} %get-tuple-element.347), channel_id=1, source_target_pairs={{0,1},{1,2},{2,3},{3,4},{4,5},{5,6},{6,7},{7,8},{8,9},{9,10},{10,1... | collective-permute-start | bytes 6200 | tf_op jit(solution)/shard_map/ppermute | solution.py:23
  107.7 7.8 %collective-permute-start.3 = (f32[2,258,1]{2,1,0:T(8,128)S(1)}, f32[2,258,1]{2,1,0:T(8,128)S(1)}, u32[]{:S(2)}, u32[]{:S(2)}) collective-permute-start(f32[2,258,1]{2,1,0:T(8,128)S(1)} %get-tuple-element.348), channel_id=1, source_target_pairs={{1,0},{2,1},{3,2},{4,3},{5,4},{6,5},{7,6},{8,7},{9,8},{10,9},{11,1... | collective-permute-start | bytes 6200 | tf_op jit(solution)/shard_map/ppermute | solution.py:24
where the time goes:
time: 261 us; the launch traced here: 259 us
  matrix products  149 us (57%)
  local copies, waits for them, and re-layouts  30.6 us (12%)
  starting transfers between devices  27.9 us (11%)
  other arithmetic  18.7 us (7%)
  loops' own time  18 us (7%)
  waiting for transfers between devices  8.94 us (3%)
  blocking collectives  4.98 us (2%)
    dot_general x16, matrix products, interpolate(): jnp.dot(row_weight, both_fields, precision=lax.Precision.HIGHEST, preferr...  101 us
    dot_general x8, matrix products, add_block(): lax.dot_general(spread, owner_hot, (((1,), (0,)), ((), ())), precision=la...  42.7 us
    ppermute x2, starting transfers between devices, extended(): before = lax.ppermute(last, axis, up)  13.2 us
    another operation x1, loops' own time, shards(): lax.map(one_block, jnp.arange(count // block_size, dtype=jnp.int32))  12 us
    dynamic_slice x16, local copies, waits for them, and re-layouts, shards(): lax.map(one_block, jnp.arange(count // block_size, dtype=jnp.int32))  10.7 us
    all_to_all x1, starting transfers between devices, turned_blocks(): lax.all_to_all(pieces, axes[k], split_axis=k, concat_axis=k, tiled=True)  10.5 us
    reduce_sum x16, other arithmetic, interpolate(): speed_first = jnp.sum(rows_mixed[:, :padded_width] * col_weight, axis=1)  8.71 us
    ppermute x2, waiting for transfers between devices, extended(): after = lax.ppermute(initial, axis, down)  5.91 us
  transfers between devices with their start and end apart: 5, of which 4 were waited for; matrix products, arithmetic and copies ran while one was open for 1% of the time, Pallas kernels for 0%

commit v1 on v0

v1 whole, which is shorter than its diff:
```python
import functools

import jax
import jax.numpy as jnp
from jax import lax
from jax.experimental import pallas as pl
from jax.experimental.pallas import tpu as pltpu
from jax.sharding import PartitionSpec as P

AXES = ("gx", "gy", "gz")
MESH = pl.DeviceIdType.MESH
F32, BF16, I32 = jnp.float32, jnp.bfloat16, jnp.int32
CAP = 256
CHUNK = 1024
LANES = 128
step_length = 0.5


def quad_weights(frac):
    return (0.5 * frac * (frac - 1.0), 1.0 - frac * frac, 0.5 * frac * (frac + 1.0))


def two_parts(x):
    high = x.astype(BF16)
    return high, (x - high.astype(F32)).astype(BF16)


def sort_kernel(
    part_ref, key_ref, a_ref, b_ref, vel_ref, out_ref, cell_ref, turned_ref,
    pos_ref, acc_ref, sorted_ref, sorted_cell_ref, table_ref, table_smem, sem,
):
    count = part_ref.shape[1]
    owners = out_ref.shape[0]
    chunks = count // CHUNK
    turned_ref[0] = vel_ref[0].T
    turned_ref[1] = vel_ref[1].T

    owner_ids = lax.broadcasted_iota(I32, (owners, CHUNK), 0)

    def count_chunk(i, total):
        keys = key_ref[:, pl.ds(pl.multiple_of(i * CHUNK, CHUNK), CHUNK)]
        hot = (owner_ids == keys).astype(F32)
        for j in range(CHUNK // LANES):
            total = total + hot[:, j * LANES : (j + 1) * LANES]
        return total

    spread = lax.fori_loop(0, chunks, count_chunk, jnp.zeros((owners, LANES), F32))
    hist = jnp.broadcast_to(jnp.sum(spread, axis=1, keepdims=True), (owners, owners))
    row = lax.broadcasted_iota(I32, (owners, owners), 0)
    col = lax.broadcasted_iota(I32, (owners, owners), 1)
    below = (col < row).astype(F32).astype(BF16)
    starts = jnp.dot(below, hist.astype(BF16), preferred_element_type=F32)
    table_ref[0:8, :] = starts.T[0:8, :].astype(I32)
    table_ref[8:16, :] = hist.T[0:8, :].astype(I32)
    copy = pltpu.make_async_copy(table_ref, table_smem, sem)
    copy.start()

    upper = (
        lax.broadcasted_iota(I32, (CAP, CAP), 0) <= lax.broadcasted_iota(I32, (CAP, CAP), 1)
    ).astype(F32).astype(BF16)
    block_ids = lax.broadcasted_iota(I32, (owners, CAP), 0)

    def rank_chunk(i, base):
        for j in range(CHUNK // CAP):
            at = pl.ds(pl.multiple_of(i * CHUNK + j * CAP, CAP), CAP)
            hot = (block_ids == key_ref[:, at]).astype(F32)
            upto = jnp.dot(hot.astype(BF16), upper, preferred_element_type=F32)
            places = jnp.sum(hot * (upto + base), axis=0, keepdims=True) - 1.0
            pos_ref[:, at] = places.astype(I32)
            base = base + upto[:, CAP - 1 : CAP]
        return base

    lax.fori_loop(0, chunks, rank_chunk, starts[:, 0:1])

    acc_ref[...] = jnp.zeros_like(acc_ref)
    lane_ids = lax.broadcasted_iota(I32, (CAP, CHUNK), 0)
    page_ids = lax.broadcasted_iota(I32, (32, CHUNK), 0)

    def place_chunk(i, carry):
        at = pl.ds(pl.multiple_of(i * CHUNK, CHUNK), CHUNK)
        pos = pos_ref[:, at]
        page = pos >> 8
        lane_hot = (lane_ids == (pos & 255)).astype(F32).astype(BF16)
        values = jnp.concatenate(two_parts(part_ref[:, at]), axis=0)
        page16 = jnp.broadcast_to(page, (16, CHUNK)).astype(F32).astype(BF16)
        zero = jnp.zeros((16, CHUNK), BF16)
        rows = [jnp.where(page16 == BF16(h), values, zero) for h in range(32)]
        page_hot = (page_ids == page)
        rows.append(jnp.where(page_hot, a_ref[:, at].astype(F32), 0.0).astype(BF16))
        rows.append(jnp.where(page_hot, b_ref[:, at].astype(F32), 0.0).astype(BF16))
        acc_ref[...] += lax.dot_general(
            jnp.concatenate(rows, axis=0), lane_hot, (((1,), (1,)), ((), ())),
            preferred_element_type=F32,
        )
        return carry

    lax.fori_loop(0, chunks, place_chunk, 0)

    cells = (acc_ref[512:544, :] * 128.0 + acc_ref[544:576, :]).astype(I32)
    for h in range(32):
        both = acc_ref[16 * h : 16 * h + 8, :] + acc_ref[16 * h + 8 : 16 * h + 16, :]
        for j in range(2):
            sorted_ref[2 * h + j] = both[:, j * LANES : (j + 1) * LANES]
            sorted_cell_ref[2 * h + j] = cells[h : h + 1, j * LANES : (j + 1) * LANES]
    for j in range(64, 67):
        sorted_ref[j] = jnp.zeros((8, LANES), F32)
        sorted_cell_ref[j] = jnp.zeros((1, LANES), I32)
    copy.wait()

    lanes8 = lax.broadcasted_iota(I32, (8, LANES), 1)
    lanes1 = lax.broadcasted_iota(I32, (1, LANES), 1)

    def expand(d, carry):
        start = table_smem[0, d]
        live = table_smem[8, d]
        page = start >> 7
        shift = start & 127
        turn = (LANES - shift) & 127
        head8, head1 = lanes8 < LANES - shift, lanes1 < LANES - shift
        rolled = [pltpu.roll(sorted_ref[page + j], turn, 1) for j in range(3)]
        cell_rolled = [pltpu.roll(sorted_cell_ref[page + j], turn, 1) for j in range(3)]
        for j in range(2):
            here = slice(j * LANES, (j + 1) * LANES)
            value = jnp.where(head8, rolled[j], rolled[j + 1])
            out_ref[d, :, here] = jnp.where(lanes8 < live - j * LANES, value, 0.0)
            cell = jnp.where(head1, cell_rolled[j], cell_rolled[j + 1])
            cell_ref[d, :, here] = jnp.where(lanes1 < live - j * LANES, cell, -1)
        return carry

    lax.fori_loop(0, owners, expand, 0, unroll=8)


def sorted_blocks(particles, dest_key, cell_a, cell_b, velocity, owners):
    count = particles.shape[1]
    tile = velocity.shape
    vmem = pl.BlockSpec(memory_space=pltpu.VMEM)
    return pl.pallas_call(
        sort_kernel,
        out_shape=(
            jax.ShapeDtypeStruct((owners, 8, CAP), F32),
            jax.ShapeDtypeStruct((owners, 1, CAP), I32),
            jax.ShapeDtypeStruct((tile[0], tile[2], tile[1]), F32),
        ),
        in_specs=[vmem] * 5,
        out_specs=(vmem,) * 3,
        scratch_shapes=[
            pltpu.VMEM((1, count), I32),
            pltpu.VMEM((576, CAP), F32),
            pltpu.VMEM((67, 8, LANES), F32),
            pltpu.VMEM((67, 1, LANES), I32),
            pltpu.VMEM((16, LANES), I32),
            pltpu.SMEM((16, LANES), I32),
            pltpu.SemaphoreType.DMA,
        ],
        name="sort",
    )(particles, dest_key.reshape(1, -1), cell_a.reshape(1, -1), cell_b.reshape(1, -1), velocity)


def exchange_kernel(
    sizes, out_ref, cell_ref, vel_ref, turned_ref,
    in_ref, in_cell_ref, rows_ref, cols_ref,
    send_sem, recv_sem, cell_send, cell_recv, halo_send, halo_recv, own_sem,
):
    nx, ny, nz = sizes
    total = nx * ny * nz
    x, y, z = (lax.axis_index(a) for a in AXES)
    me = (x * ny + y) * nz + z

    own = pltpu.make_async_copy(out_ref.at[me], in_ref.at[me], own_sem.at[0])
    own_cell = pltpu.make_async_copy(cell_ref.at[me], in_cell_ref.at[me], own_sem.at[1])
    own.start()
    own_cell.start()

    tiles = ny * nz
    tile = y * nz + z
    height = vel_ref.shape[1]
    width = vel_ref.shape[2]
    halos = []
    n = 0
    for i, dx in enumerate((1, -1)):
        to_x = lax.rem(x + dx + nx, nx)
        edge = vel_ref.at[:, pl.ds(height - 8 if dx == 1 else 0, 8), :]
        for j, dt in enumerate((1, 0, -1)):
            to_t = lax.rem(tile + dt + tiles, tiles)
            halos.append((edge, rows_ref.at[3 * i + j], to_x, to_t, n))
            n += 1
    for i, dt in enumerate((1, -1)):
        edge = turned_ref.at[:, pl.ds(width - 8 if dt == 1 else 0, 8), :]
        to_t = lax.rem(tile + dt + tiles, tiles)
        halos.append((edge, cols_ref.at[i], x, to_t, n))
        n += 1
    halo_copies = [
        pltpu.make_async_remote_copy(
            src_ref=src, dst_ref=dst, send_sem=halo_send.at[k], recv_sem=halo_recv.at[k],
            device_id=(to_x, to_t // nz, lax.rem(to_t, nz)), device_id_type=MESH,
        )
        for src, dst, to_x, to_t, k in halos
    ]
    for c in halo_copies:
        c.start()

    def send(k, carry):
        dx, dy, dz = k // (ny * nz), lax.rem(k // nz, ny), lax.rem(k, nz)
        to_x = lax.rem(x + dx, nx)
        to_yy = lax.rem(y // 4 + dy // 4, ny // 4)
        to_yx = lax.rem(lax.rem(y, 4) + lax.rem(dy, 4), 4)
        to_y = to_yy * 4 + to_yx
        to_z = lax.rem(z + dz, nz)
        there = (to_x * ny + to_y) * nz + to_z
        device = (to_x, to_y, to_z)
        pltpu.make_async_remote_copy(
            src_ref=out_ref.at[there], dst_ref=in_ref.at[me], send_sem=send_sem, recv_sem=recv_sem,
            device_id=device, device_id_type=MESH,
        ).start()
        pltpu.make_async_remote_copy(
            src_ref=cell_ref.at[there], dst_ref=in_cell_ref.at[me], send_sem=cell_send, recv_sem=cell_recv,
            device_id=device, device_id_type=MESH,
        ).start()
        return carry

    lax.fori_loop(1, total, send, 0)
    some, some_cell = in_ref.at[pl.ds(0, total - 1)], in_cell_ref.at[pl.ds(0, total - 1)]
    own.wait()
    own_cell.wait()
    for c in halo_copies:
        c.wait()
    pltpu.make_async_copy(some, some, recv_sem).wait()
    pltpu.make_async_copy(some_cell, some_cell, cell_recv).wait()
    pltpu.make_async_copy(some, some, send_sem).wait()
    pltpu.make_async_copy(some_cell, some_cell, cell_send).wait()


def exchanged(blocks, cells, velocity, turned, sizes):
    parts, height, width = velocity.shape
    vmem = pl.BlockSpec(memory_space=pltpu.VMEM)
    dma = pltpu.SemaphoreType.DMA
    return pl.pallas_call(
        functools.partial(exchange_kernel, sizes),
        out_shape=(
            jax.ShapeDtypeStruct(blocks.shape, F32),
            jax.ShapeDtypeStruct(cells.shape, I32),
            jax.ShapeDtypeStruct((6, parts, 8, width), F32),
            jax.ShapeDtypeStruct((2, parts, 8, height), F32),
        ),
        in_specs=[vmem] * 4,
        out_specs=(vmem,) * 4,
        scratch_shapes=[dma, dma, dma, dma, dma((8,)), dma((8,)), dma((2,))],
        compiler_params=pltpu.CompilerParams(has_side_effects=True),
        name="exchange",
    )(blocks, cells, velocity, turned)


def interpolate_kernel(
    sizes, in_ref, cell_ref, turned_ref, rows_ref, cols_ref, out_ref, out_cell_ref,
    high_ref, low_ref, up_ref, down_ref,
):
    nx, ny, nz = sizes
    width, height = turned_ref.shape[1], turned_ref.shape[2]
    group = in_ref.shape[0]

    @pl.when(pl.program_id(0) == 0)
    def prepare():
        x = lax.axis_index("gx")
        tile = lax.axis_index("gy") * nz + lax.axis_index("gz")
        has_left, has_right = tile > 0, tile < ny * nz - 1
        left = [jnp.where(has_left, cols_ref[0, c, 7:8, :], 0.0) for c in range(2)]
        right = [jnp.where(has_right, cols_ref[1, c, 0:1, :], 0.0) for c in range(2)]
        zeros = jnp.zeros((4, height), F32)
        sides = jnp.concatenate([left[0], right[0], left[1], right[1], zeros], axis=0)
        for c, at in ((0, 0), (1, width), (None, 2 * width)):
            block = sides if c is None else turned_ref[c]
            high, low = two_parts(block)
            high_ref[at : at + block.shape[0], :] = high
            low_ref[at : at + block.shape[0], :] = low
        for ref, first, row, there in ((up_ref, 0, 7, x > 0), (down_ref, 3, 0, x < nx - 1)):
            corner = []
            for c in range(2):
                line = jnp.where(there, rows_ref[first + 1, c], 0.0).T[:, row : row + 1]
                ref[c * width : (c + 1) * width, :] = jnp.broadcast_to(line, (width, LANES))
                from_left = rows_ref[first, c][row : row + 1, width - 1 : width]
                from_right = rows_ref[first + 2, c][row : row + 1, 0:1]
                corner.append(jnp.where(there & has_left, from_left, 0.0))
                corner.append(jnp.where(there & has_right, from_right, 0.0))
            ref[2 * width :, :] = jnp.broadcast_to(
                jnp.concatenate(corner + [jnp.zeros((4, 1), F32)], axis=0), (8, LANES)
            )

    row_ids = lax.broadcasted_iota(I32, (height, CAP), 0).astype(F32).astype(BF16)
    col_ids = lax.broadcasted_iota(I32, (width, CAP), 0)
    sub_ids = lax.broadcasted_iota(I32, (8, CAP), 0)

    def one_source(s, carry):
        data = in_ref[s]
        cell = cell_ref[s]
        live = cell >= 0
        node_a = jnp.where(live, cell >> 7, 2 * height)
        node_b = cell & 127
        below, same, above = quad_weights(data[0:1, :])
        left, mid, right = quad_weights(data[1:2, :])
        a16 = node_a.astype(F32).astype(BF16)
        is_same = row_ids == a16
        is_below = row_ids == a16 - BF16(1)
        is_above = row_ids == a16 + BF16(1)
        weights = []
        for part in zip(two_parts(below), two_parts(same), two_parts(above)):
            weights.append(
                jnp.where(is_below, part[0], jnp.where(is_same, part[1], jnp.where(is_above, part[2], BF16(0))))
            )
        dot = functools.partial(jnp.dot, preferred_element_type=F32)
        mixed = dot(high_ref[...], weights[0]) + dot(high_ref[...], weights[1]) + dot(low_ref[...], weights[0])
        first = node_a == 0
        edge = jnp.where(first, below, jnp.where(node_a == height - 1, above, 0.0))
        up = jnp.concatenate([up_ref[...]] * 2, axis=1)
        down = jnp.concatenate([down_ref[...]] * 2, axis=1)
        mixed = mixed + jnp.where(first, up, down) * edge
        cols = jnp.where(
            col_ids == node_b - 1, left, jnp.where(col_ids == node_b, mid, jnp.where(col_ids == node_b + 1, right, 0.0))
        )
        at_left = jnp.where(node_b == 0, left, 0.0)
        at_right = jnp.where(node_b == width - 1, right, 0.0)
        speed = []
        for c in range(2):
            inner = jnp.sum(mixed[c * width : (c + 1) * width, :] * cols, axis=0, keepdims=True)
            side = 2 * width + 2 * c
            speed.append(
                inner + mixed[side : side + 1, :] * at_left + mixed[side + 1 : side + 2, :] * at_right
            )
        shift = jnp.where(sub_ids == 2, speed[0], jnp.where(sub_ids == 3, speed[1], 0.0))
        here = pl.ds(pl.multiple_of(s * CAP, CAP), CAP)
        out_ref[:, here] = data + step_length * shift
        out_cell_ref[s] = cell
        return carry

    lax.fori_loop(0, group, one_source, 0, unroll=2)


def interpolated(blocks, cells, turned, rows, cols, sizes):
    sources = blocks.shape[0]
    parts, width, height = turned.shape
    group = 8
    whole = pl.BlockSpec(memory_space=pltpu.VMEM)
    return pl.pallas_call(
        functools.partial(interpolate_kernel, sizes),
        grid=(sources // group,),
        out_shape=(
            jax.ShapeDtypeStruct((8, sources * CAP), F32),
            jax.ShapeDtypeStruct((sources, 1, CAP), I32),
        ),
        in_specs=[
            pl.BlockSpec((group, 8, CAP), lambda i: (i, 0, 0)),
            pl.BlockSpec((group, 1, CAP), lambda i: (i, 0, 0)),
            whole, whole, whole,
        ],
        out_specs=(
            pl.BlockSpec((8, group * CAP), lambda i: (0, i)),
            pl.BlockSpec((group, 1, CAP), lambda i: (i, 0, 0)),
        ),
        scratch_shapes=[
            pltpu.VMEM((2 * width + 8, height), BF16),
            pltpu.VMEM((2 * width + 8, height), BF16),
            pltpu.VMEM((2 * width + 8, LANES), F32),
            pltpu.VMEM((2 * width + 8, LANES), F32),
        ],
        name="interpolate",
    )(blocks, cells, turned, rows, cols)


def shards(sizes, particles, dest_key, cell_a, cell_b, velocity):
    owners = sizes[0] * sizes[1] * sizes[2]
    blocks, cells, turned = sorted_blocks(particles, dest_key, cell_a, cell_b, velocity, owners)
    arrived, arrived_cells, rows, cols = exchanged(blocks, cells, velocity, turned, sizes)
    binned, binned_cell = interpolated(arrived, arrived_cells, turned, rows, cols, sizes)
    return binned, binned_cell.reshape(-1)


def solution(mesh):
    sizes = tuple(mesh.shape[a] for a in AXES)
    in_specs = (P(None, AXES), P(AXES), P(AXES), P(AXES), P(None, "gx", ("gy", "gz")))
    out_specs = (P(None, AXES), P(AXES))
    return jax.shard_map(
        functools.partial(shards, sizes), mesh=mesh, in_specs=in_specs, out_specs=out_specs, check_vma=False
    )
```

time: 261 us -> 83.6 us (0.32)
  the two profiles are of different devices: /device:TPU:43 before, /device:TPU:1 now
where the time goes in v1:
time: 83.6 us; the launch traced here: 83.4 us
  Pallas kernels  82.8 us (99%)
    pallas_call x1, Pallas kernels, exchanged(): pl.pallas_call(functools.partial(exchange_kernel, sizes), out_shape=(jax....  35.2 us
    pallas_call x1, Pallas kernels, interpolated(): pl.pallas_call(functools.partial(interpolate_kernel, sizes), grid=(source...  34.9 us
    pallas_call x1, Pallas kernels, sorted_blocks(): pl.pallas_call(sort_kernel, out_shape=(jax.ShapeDtypeStruct((owners, 8, C...  12.7 us

profile of v1, /device:TPU:1, one launch (start us, length us, event | category | flops | bytes accessed | tf_op | source)
XLA Modules:
  0.0 83.4 jit_solution(4334355128875656201)
XLA Ops:
  0.6 12.7 %sort.1 = (f32[128,8,256]{2,1,0:T(8,128)}, s32[128,1,256]{2,1,0:T(1,128)}, f32[2,128,256]{2,1,0:T(8,128)}) custom-call(f32[8,8192]{1,0:T(8,128)} %part_ref.1, s32[1,8192]{1,0:T(1,128)} %bitcast.4, s32[1,8192]{1,0:T(1,128)} %bitcast.5, s32[1,8192]{1,0:T(1,128)} %bitcast.6, f32[2,256,128]{2,1,0:T(8,128)} %vel_ref.3), custom_call_target="tpu_custom_call" | custom-call | tf_op jit(solution)/shard_map/sort/pallas_call | solution.py:137
  13.3 35.2 %exchange.1 = (f32[128,8,256]{2,1,0:T(8,128)}, s32[128,1,256]{2,1,0:T(1,128)}, f32[6,2,8,128]{3,2,1,0:T(8,128)}, f32[2,2,8,256]{3,2,1,0:T(8,128)}) custom-call(f32[128,8,256]{2,1,0:T(8,128)} %get-tuple-element.11.out_ref, s32[128,1,256]{2,1,0:T(1,128)} %get-tuple-element.12.cell_ref, f32[2,256,128]{2,1,0:T(8,128)} %vel_ref.3, ...), custom_call_target="tpu_custom_call" | custom-call | tf_op jit(solution)/shard_map/exchange/pallas_call | solution.py:237
  48.6 34.9 %interpolate.1 = (f32[8,32768]{1,0:T(8,128)}, s32[128,1,256]{2,1,0:T(1,128)}) custom-call(f32[128,8,256]{2,1,0:T(8,128)} %get-tuple-element.14.in_ref, s32[128,1,256]{2,1,0:T(1,128)} %get-tuple-element.15.cell_ref, f32[2,128,256]{2,1,0:T(8,128)} %get-tuple-element.13.turned_ref, f32[6,2,8,128]{3,2,1,0:T(8,128)} %get-tuple-element.16.rows_ref, ...), custom_call_target="tpu_custom_call" | custom-call | tf_op jit(solution)/shard_map/interpolate/pallas_call | solution.py:342

commit v2 on v1

v2 whole, which is shorter than its diff:
```python
import functools

import jax
import jax.numpy as jnp
from jax import lax
from jax.experimental import pallas as pl
from jax.experimental.pallas import tpu as pltpu
from jax.sharding import PartitionSpec as P

AXES = ("gx", "gy", "gz")
MESH = pl.DeviceIdType.MESH
F32, BF16, I32 = jnp.float32, jnp.bfloat16, jnp.int32
CAP = 256
CHUNK = 1024
LANES = 128
step_length = 0.5


def quad_weights(frac):
    return (0.5 * frac * (frac - 1.0), 1.0 - frac * frac, 0.5 * frac * (frac + 1.0))


def two_parts(x):
    high = x.astype(BF16)
    return high, (x - high.astype(F32)).astype(BF16)


def sort_phase(
    part_ref, key_ref, a_ref, b_ref,
    pos_ref, acc_ref, sorted_ref, sorted_cell_ref, table_ref, table_smem, sem, owners, between,
):
    count = part_ref.shape[1]
    chunks = count // CHUNK

    owner_ids = lax.broadcasted_iota(I32, (owners, CHUNK), 0)

    def count_chunk(i, total):
        keys = key_ref[:, pl.ds(pl.multiple_of(i * CHUNK, CHUNK), CHUNK)]
        hot = (owner_ids == keys).astype(F32)
        for j in range(CHUNK // LANES):
            total = total + hot[:, j * LANES : (j + 1) * LANES]
        return total

    spread = lax.fori_loop(0, chunks, count_chunk, jnp.zeros((owners, LANES), F32))
    hist = jnp.broadcast_to(jnp.sum(spread, axis=1, keepdims=True), (owners, owners))
    row = lax.broadcasted_iota(I32, (owners, owners), 0)
    col = lax.broadcasted_iota(I32, (owners, owners), 1)
    below = (col < row).astype(F32).astype(BF16)
    starts = jnp.dot(below, hist.astype(BF16), preferred_element_type=F32)
    table_ref[0:8, :] = starts.T[0:8, :].astype(I32)
    table_ref[8:16, :] = hist.T[0:8, :].astype(I32)
    copy = pltpu.make_async_copy(table_ref, table_smem, sem)
    copy.start()

    upper = (
        lax.broadcasted_iota(I32, (CAP, CAP), 0) <= lax.broadcasted_iota(I32, (CAP, CAP), 1)
    ).astype(F32).astype(BF16)
    block_ids = lax.broadcasted_iota(I32, (owners, CAP), 0)

    def rank_chunk(i, base):
        for j in range(CHUNK // CAP):
            at = pl.ds(pl.multiple_of(i * CHUNK + j * CAP, CAP), CAP)
            hot = (block_ids == key_ref[:, at]).astype(F32)
            upto = jnp.dot(hot.astype(BF16), upper, preferred_element_type=F32)
            places = jnp.sum(hot * (upto + base), axis=0, keepdims=True) - 1.0
            pos_ref[:, at] = places.astype(I32)
            base = base + upto[:, CAP - 1 : CAP]
        return base

    lax.fori_loop(0, chunks, rank_chunk, starts[:, 0:1])
    between()

    acc_ref[...] = jnp.zeros_like(acc_ref)
    lane_ids = lax.broadcasted_iota(I32, (CAP, CHUNK), 0)
    page_ids = lax.broadcasted_iota(I32, (32, CHUNK), 0)

    def place_chunk(i, carry):
        at = pl.ds(pl.multiple_of(i * CHUNK, CHUNK), CHUNK)
        pos = pos_ref[:, at]
        page = pos >> 8
        lane_hot = (lane_ids == (pos & 255)).astype(F32).astype(BF16)
        values = jnp.concatenate(two_parts(part_ref[:, at]), axis=0)
        page16 = jnp.broadcast_to(page, (16, CHUNK)).astype(F32).astype(BF16)
        zero = jnp.zeros((16, CHUNK), BF16)
        rows = [jnp.where(page16 == BF16(h), values, zero) for h in range(32)]
        page_hot = (page_ids == page)
        rows.append(jnp.where(page_hot, a_ref[:, at].astype(F32), 0.0).astype(BF16))
        rows.append(jnp.where(page_hot, b_ref[:, at].astype(F32), 0.0).astype(BF16))
        acc_ref[...] += lax.dot_general(
            jnp.concatenate(rows, axis=0), lane_hot, (((1,), (1,)), ((), ())),
            preferred_element_type=F32,
        )
        return carry

    lax.fori_loop(0, chunks, place_chunk, 0)

    cells = (acc_ref[512:544, :] * 128.0 + acc_ref[544:576, :]).astype(I32)
    for h in range(32):
        both = acc_ref[16 * h : 16 * h + 8, :] + acc_ref[16 * h + 8 : 16 * h + 16, :]
        for j in range(2):
            sorted_ref[2 * h + j] = both[:, j * LANES : (j + 1) * LANES]
            sorted_cell_ref[2 * h + j] = cells[h : h + 1, j * LANES : (j + 1) * LANES]
    for j in range(64, 67):
        sorted_ref[j] = jnp.zeros((8, LANES), F32)
        sorted_cell_ref[j] = jnp.zeros((1, LANES), I32)
    copy.wait()


def expand(d, sorted_ref, sorted_cell_ref, table_smem, send_ref, send_cell_ref):
    lanes8 = lax.broadcasted_iota(I32, (8, LANES), 1)
    lanes1 = lax.broadcasted_iota(I32, (1, LANES), 1)
    start = jnp.clip(table_smem[0, d], 0, LANES * (sorted_ref.shape[0] - 3))
    live = table_smem[8, d]
    page = start >> 7
    shift = start & 127
    turn = (LANES - shift) & 127
    head8, head1 = lanes8 < LANES - shift, lanes1 < LANES - shift
    rolled = [pltpu.roll(sorted_ref[page + j], turn, 1) for j in range(3)]
    cell_rolled = [pltpu.roll(sorted_cell_ref[page + j], turn, 1) for j in range(3)]
    for j in range(2):
        here = slice(j * LANES, (j + 1) * LANES)
        value = jnp.where(head8, rolled[j], rolled[j + 1])
        send_ref[d, :, here] = jnp.where(lanes8 < live - j * LANES, value, 0.0)
        cell = jnp.where(head1, cell_rolled[j], cell_rolled[j + 1])
        send_cell_ref[d, :, here] = jnp.where(lanes1 < live - j * LANES, cell, -1)


def prepare_field(sizes, turned_ref, rows_ref, cols_ref, high_ref, low_ref, up_ref, down_ref):
    nx, ny, nz = sizes
    width, height = turned_ref.shape[1], turned_ref.shape[2]
    x = lax.axis_index("gx")
    tile = lax.axis_index("gy") * nz + lax.axis_index("gz")
    has_left, has_right = tile > 0, tile < ny * nz - 1
    left = [jnp.where(has_left, cols_ref[0, c, 7:8, :], 0.0) for c in range(2)]
    right = [jnp.where(has_right, cols_ref[1, c, 0:1, :], 0.0) for c in range(2)]
    zeros = jnp.zeros((4, height), F32)
    sides = jnp.concatenate([left[0], right[0], left[1], right[1], zeros], axis=0)
    for c, at in ((0, 0), (1, width), (None, 2 * width)):
        block = sides if c is None else turned_ref[c]
        high, low = two_parts(block)
        high_ref[at : at + block.shape[0], :] = high
        low_ref[at : at + block.shape[0], :] = low
    for ref, first, row, there in ((up_ref, 0, 7, x > 0), (down_ref, 3, 0, x < nx - 1)):
        corner = []
        for c in range(2):
            line = jnp.where(there, rows_ref[first + 1, c], 0.0).T[:, row : row + 1]
            ref[c * width : (c + 1) * width, :] = jnp.broadcast_to(line, (width, LANES))
            from_left = rows_ref[first, c][row : row + 1, width - 1 : width]
            from_right = rows_ref[first + 2, c][row : row + 1, 0:1]
            corner.append(jnp.where(there & has_left, from_left, 0.0))
            corner.append(jnp.where(there & has_right, from_right, 0.0))
        ref[2 * width :, :] = jnp.broadcast_to(
            jnp.concatenate(corner + [jnp.zeros((4, 1), F32)], axis=0), (8, LANES)
        )


def interpolate_source(s, out_ref, cell_ref, high_ref, low_ref, up_ref, down_ref):
    height = high_ref.shape[1]
    width = (high_ref.shape[0] - 8) // 2
    row_ids = lax.broadcasted_iota(I32, (height, CAP), 0).astype(F32).astype(BF16)
    col_ids = lax.broadcasted_iota(I32, (width, CAP), 0)
    sub_ids = lax.broadcasted_iota(I32, (8, CAP), 0)
    here = pl.ds(pl.multiple_of(s * CAP, CAP), CAP)
    data = out_ref[:, here]
    cell = cell_ref[s]
    live = cell >= 0
    node_a = jnp.where(live, cell >> 7, 2 * height)
    node_b = cell & 127
    below, same, above = quad_weights(data[0:1, :])
    left, mid, right = quad_weights(data[1:2, :])
    a16 = node_a.astype(F32).astype(BF16)
    is_same = row_ids == a16
    is_below = row_ids == a16 - BF16(1)
    is_above = row_ids == a16 + BF16(1)
    weights = []
    for part in zip(two_parts(below), two_parts(same), two_parts(above)):
        weights.append(
            jnp.where(is_below, part[0], jnp.where(is_same, part[1], jnp.where(is_above, part[2], BF16(0))))
        )
    dot = functools.partial(jnp.dot, preferred_element_type=F32)
    mixed = dot(high_ref[...], weights[0]) + dot(high_ref[...], weights[1]) + dot(low_ref[...], weights[0])
    first = node_a == 0
    edge = jnp.where(first, below, jnp.where(node_a == height - 1, above, 0.0))
    up = jnp.concatenate([up_ref[...]] * 2, axis=1)
    down = jnp.concatenate([down_ref[...]] * 2, axis=1)
    mixed = mixed + jnp.where(first, up, down) * edge
    cols = jnp.where(
        col_ids == node_b - 1, left, jnp.where(col_ids == node_b, mid, jnp.where(col_ids == node_b + 1, right, 0.0))
    )
    at_left = jnp.where(node_b == 0, left, 0.0)
    at_right = jnp.where(node_b == width - 1, right, 0.0)
    speed = []
    for c in range(2):
        inner = jnp.sum(mixed[c * width : (c + 1) * width, :] * cols, axis=0, keepdims=True)
        side = 2 * width + 2 * c
        speed.append(
            inner + mixed[side : side + 1, :] * at_left + mixed[side + 1 : side + 2, :] * at_right
        )
    shift = jnp.where(sub_ids == 2, speed[0], jnp.where(sub_ids == 3, speed[1], 0.0))
    out_ref[:, here] = data + step_length * shift


GROUP = 8


def rebin_kernel(
    sizes, part_ref, key_ref, a_ref, b_ref, vel_ref, out_ref, cell_ref,
    pos_ref, acc_ref, sorted_ref, sorted_cell_ref, table_ref, table_smem,
    send_ref, send_cell_ref, turned_ref, rows_ref, cols_ref, high_ref, low_ref, up_ref, down_ref,
    table_sem, send_sem, send_cell_sem, recv_sem, recv_cell_sem, halo_send, halo_recv,
):
    nx, ny, nz = sizes
    total = nx * ny * nz
    side = 4
    x, y, z = (lax.axis_index(a) for a in AXES)
    me = (x * ny + y) * nz + z
    tiles = ny * nz
    tile = y * nz + z
    height, width = vel_ref.shape[1], vel_ref.shape[2]

    def peer(k, sign):
        dx = lax.rem(k // tiles + nx // 2, nx)
        dy = lax.rem(k // (side * nz) + ny // side // 2, ny // side)
        dyx = lax.rem(k // nz + side // 2, side)
        dz = lax.rem(k, nz)
        if sign < 0:
            dx, dy, dyx, dz = nx - dx, ny // side - dy, side - dyx, nz - dz
        to_x = lax.rem(x + dx, nx)
        to_y = lax.rem(y // side + dy, ny // side) * side + lax.rem(lax.rem(y, side) + dyx, side)
        to_z = lax.rem(z + dz, nz)
        return (to_x * ny + to_y) * nz + to_z, (to_x, to_y, to_z)

    own = ((nx // 2) * (ny // side) + ny // side // 2) * side * nz + (side // 2) * nz

    barrier = pltpu.get_barrier_semaphore()

    def greet(k, carry):
        @pl.when(k != own)
        def tell():
            pl.semaphore_signal(barrier, inc=1, device_id=peer(k, 1)[1], device_id_type=MESH)
        return carry

    lax.fori_loop(0, total, greet, 0)
    turned_ref[0] = vel_ref[0].T
    turned_ref[1] = vel_ref[1].T

    halos = []
    for i, dx in enumerate((1, -1)):
        to_x = lax.rem(x + dx + nx, nx)
        edge = vel_ref.at[:, pl.ds(height - 8 if dx == 1 else 0, 8), :]
        for j, dt in enumerate((1, 0, -1)):
            halos.append((edge, rows_ref.at[3 * i + j], to_x, lax.rem(tile + dt + tiles, tiles)))
    for i, dt in enumerate((1, -1)):
        edge = turned_ref.at[:, pl.ds(width - 8 if dt == 1 else 0, 8), :]
        halos.append((edge, cols_ref.at[i], x, lax.rem(tile + dt + tiles, tiles)))
    halo_copies = [
        pltpu.make_async_remote_copy(
            src_ref=src, dst_ref=dst, send_sem=halo_send.at[k], recv_sem=halo_recv.at[k],
            device_id=(to_x, to_t // nz, lax.rem(to_t, nz)), device_id_type=MESH,
        )
        for k, (src, dst, to_x, to_t) in enumerate(halos)
    ]

    def between():
        pl.semaphore_wait(barrier, total - 1)
        for c in halo_copies:
            c.start()

    sort_phase(
        part_ref, key_ref, a_ref, b_ref, pos_ref, acc_ref, sorted_ref, sorted_cell_ref,
        table_ref, table_smem, table_sem, total, between,
    )

    mine = pl.ds(pl.multiple_of(me * CAP, CAP), CAP)

    def send_group(g):
        def send(i, carry):
            k = g * GROUP + i
            there, device = peer(k, 1)

            @pl.when(k != own)
            def remote():
                pltpu.make_async_remote_copy(
                    src_ref=send_ref.at[there], dst_ref=out_ref.at[:, mine], send_sem=send_sem,
                    recv_sem=recv_sem.at[g], device_id=device, device_id_type=MESH,
                ).start()
                pltpu.make_async_remote_copy(
                    src_ref=send_cell_ref.at[there], dst_ref=cell_ref.at[me], send_sem=send_cell_sem,
                    recv_sem=recv_cell_sem.at[g], device_id=device, device_id_type=MESH,
                ).start()

            @pl.when(k == own)
            def local():
                pltpu.make_async_copy(send_ref.at[there], out_ref.at[:, mine], recv_sem.at[g]).start()
                pltpu.make_async_copy(send_cell_ref.at[there], cell_ref.at[me], recv_cell_sem.at[g]).start()

            return carry

        lax.fori_loop(0, GROUP, send, 0)

    def expand_group(g, carry):
        for i in range(GROUP):
            there = peer(g * GROUP + i, 1)[0]
            expand(there, sorted_ref, sorted_cell_ref, table_smem, send_ref, send_cell_ref)

        @pl.when(g > 0)
        def before():
            send_group(g - 1)

        return carry

    groups = total // GROUP
    lax.fori_loop(0, groups, expand_group, 0)
    send_group(groups - 1)

    for c in halo_copies:
        c.wait()
    prepare_field(sizes, turned_ref, rows_ref, cols_ref, high_ref, low_ref, up_ref, down_ref)

    def finish_group(g, carry):
        blocks = out_ref.at[:, pl.ds(0, GROUP * CAP)]
        pltpu.make_async_copy(blocks, blocks, recv_sem.at[g]).wait()
        few = cell_ref.at[pl.ds(0, GROUP)]
        pltpu.make_async_copy(few, few, recv_cell_sem.at[g]).wait()

        def one(i, inner):
            source = peer(g * GROUP + i, -1)[0]
            interpolate_source(source, out_ref, cell_ref, high_ref, low_ref, up_ref, down_ref)
            return inner

        lax.fori_loop(0, GROUP, one, 0, unroll=2)
        return carry

    lax.fori_loop(0, groups, finish_group, 0)
    some = send_ref.at[pl.ds(0, total - 1)]
    some_cell = send_cell_ref.at[pl.ds(0, total - 1)]
    pltpu.make_async_copy(some, some, send_sem).wait()
    pltpu.make_async_copy(some_cell, some_cell, send_cell_sem).wait()


def shards(sizes, particles, dest_key, cell_a, cell_b, velocity):
    owners = sizes[0] * sizes[1] * sizes[2]
    count = particles.shape[1]
    parts, height, width = velocity.shape
    vmem = pl.BlockSpec(memory_space=pltpu.VMEM)
    dma = pltpu.SemaphoreType.DMA
    groups = owners // GROUP
    binned, binned_cell = pl.pallas_call(
        functools.partial(rebin_kernel, sizes),
        out_shape=(
            jax.ShapeDtypeStruct((8, owners * CAP), F32),
            jax.ShapeDtypeStruct((owners, 1, CAP), I32),
        ),
        in_specs=[vmem] * 5,
        out_specs=(vmem,) * 2,
        scratch_shapes=[
            pltpu.VMEM((1, count), I32),
            pltpu.VMEM((576, CAP), F32),
            pltpu.VMEM((67, 8, LANES), F32),
            pltpu.VMEM((67, 1, LANES), I32),
            pltpu.VMEM((16, LANES), I32),
            pltpu.SMEM((16, LANES), I32),
            pltpu.VMEM((owners, 8, CAP), F32),
            pltpu.VMEM((owners, 1, CAP), I32),
            pltpu.VMEM((parts, width, height), F32),
            pltpu.VMEM((6, parts, 8, width), F32),
            pltpu.VMEM((2, parts, 8, height), F32),
            pltpu.VMEM((2 * width + 8, height), BF16),
            pltpu.VMEM((2 * width + 8, height), BF16),
            pltpu.VMEM((2 * width + 8, LANES), F32),
            pltpu.VMEM((2 * width + 8, LANES), F32),
            dma, dma, dma, dma((groups,)), dma((groups,)), dma((8,)), dma((8,)),
        ],
        compiler_params=pltpu.CompilerParams(collective_id=0, has_side_effects=True),
        name="rebin",
    )(particles, dest_key.reshape(1, -1), cell_a.reshape(1, -1), cell_b.reshape(1, -1), velocity)
    return binned, binned_cell.reshape(-1)


def solution(mesh):
    sizes = tuple(mesh.shape[a] for a in AXES)
    in_specs = (P(None, AXES), P(AXES), P(AXES), P(AXES), P(None, "gx", ("gy", "gz")))
    out_specs = (P(None, AXES), P(AXES))
    return jax.shard_map(
        functools.partial(shards, sizes), mesh=mesh, in_specs=in_specs, out_specs=out_specs, check_vma=False
    )
```

time: 83.6 us -> 94.1 us (1.13)
  the two profiles are of different devices: /device:TPU:1 before, /device:TPU:47 now
where the time goes in v2:
time: 94.1 us; the launch traced here: 94 us
  Pallas kernels  90.4 us (96%)
  local copies, waits for them, and re-layouts  2.97 us (3%)
    pallas_call x1, Pallas kernels, shards(): pl.pallas_call(functools.partial(rebin_kernel, sizes), out_shape=(jax.Sha...  90.4 us
    unnamed x4, local copies, waits for them, and re-layouts  2.97 us

profile of v2, /device:TPU:47, one launch (start us, length us, event | category | flops | bytes accessed | tf_op | source)
XLA Modules:
  0.0 94.0 jit_solution(16933257630447906492)
XLA Ops:
  0.6 90.4 %rebin.1 = (f32[8,32768]{1,0:T(8,128)}, s32[128,1,256]{2,1,0:T(1,128)}) custom-call(f32[8,8192]{1,0:T(8,128)} %part_ref.1, s32[1,8192]{1,0:T(1,128)} %bitcast.5, s32[1,8192]{1,0:T(1,128)} %bitcast.6, s32[1,8192]{1,0:T(1,128)} %bitcast.7, f32[2,256,128]{2,1,0:T(8,128)} %vel_ref.1), custom_call_target="tpu_custom_call" | custom-call | tf_op jit(solution)/shard_map/rebin/pallas_call | solution.py:348
  91.0 0.0 copy-start
  91.0 2.3 %copy.9 = f32[8,32768]{1,0:T(8,128)} copy(f32[8,32768]{1,0:T(8,128)} %get-tuple-element.8) | data formatting | bytes 2097152
  93.3 0.0 copy-done
  93.3 0.7 copy.10
Async XLA Ops:
  91.0 2.3 %copy-start = (s32[128,1,256]{2,1,0:T(1,128)S(1)}, s32[128,1,256]{2,1,0:T(1,128)}, u32[]{:S(2)}) copy-start(s32[128,1,256]{2,1,0:T(1,128)} %get-tuple-element.5) | copy-start | bytes 393220

commit v3 on v2

--- a/solution.py
+++ b/solution.py
@@ -125,7 +125,7 @@
         send_cell_ref[d, :, here] = jnp.where(lanes1 < live - j * LANES, cell, -1)
 
 
-def prepare_field(sizes, turned_ref, rows_ref, cols_ref, high_ref, low_ref, up_ref, down_ref):
+def prepare_field(sizes, turned_ref, rows_ref, cols_ref, field_ref):
     nx, ny, nz = sizes
     width, height = turned_ref.shape[1], turned_ref.shape[2]
     x = lax.axis_index("gx")
@@ -138,125 +138,180 @@
     for c, at in ((0, 0), (1, width), (None, 2 * width)):
         block = sides if c is None else turned_ref[c]
         high, low = two_parts(block)
-        high_ref[at : at + block.shape[0], :] = high
-        low_ref[at : at + block.shape[0], :] = low
-    for ref, first, row, there in ((up_ref, 0, 7, x > 0), (down_ref, 3, 0, x < nx - 1)):
+        here = slice(at, at + block.shape[0])
+        field_ref[here, 0:height] = high
+        field_ref[here, height : 2 * height] = high
+        field_ref[here, 2 * height : 3 * height] = low
+    lane = lax.broadcasted_iota(I32, (1, LANES), 1)
+    pieces = [[], [], []]
+    for first, row, there in ((0, 7, x > 0), (3, 0, x < nx - 1)):
+        for c in range(2):
+            tile8 = jnp.where(there, rows_ref[first + 1, c], 0.0)
+            pieces[c].append(jnp.broadcast_to(tile8.T[:, row : row + 1], (width, LANES)))
         corner = []
         for c in range(2):
-            line = jnp.where(there, rows_ref[first + 1, c], 0.0).T[:, row : row + 1]
-            ref[c * width : (c + 1) * width, :] = jnp.broadcast_to(line, (width, LANES))
             from_left = rows_ref[first, c][row : row + 1, width - 1 : width]
             from_right = rows_ref[first + 2, c][row : row + 1, 0:1]
             corner.append(jnp.where(there & has_left, from_left, 0.0))
             corner.append(jnp.where(there & has_right, from_right, 0.0))
-        ref[2 * width :, :] = jnp.broadcast_to(
-            jnp.concatenate(corner + [jnp.zeros((4, 1), F32)], axis=0), (8, LANES)
-        )
-
-
-def interpolate_source(s, out_ref, cell_ref, high_ref, low_ref, up_ref, down_ref):
-    height = high_ref.shape[1]
-    width = (high_ref.shape[0] - 8) // 2
-    row_ids = lax.broadcasted_iota(I32, (height, CAP), 0).astype(F32).astype(BF16)
-    col_ids = lax.broadcasted_iota(I32, (width, CAP), 0)
-    sub_ids = lax.broadcasted_iota(I32, (8, CAP), 0)
-    here = pl.ds(pl.multiple_of(s * CAP, CAP), CAP)
-    data = out_ref[:, here]
-    cell = cell_ref[s]
-    live = cell >= 0
-    node_a = jnp.where(live, cell >> 7, 2 * height)
+        corner = jnp.concatenate(corner + [jnp.zeros((4, 1), F32)], axis=0)
+        pieces[2].append(jnp.broadcast_to(corner, (8, LANES)))
+    for c in range(3):
+        rows = pieces[c][0].shape[0]
+        here = slice(c * width, c * width + rows)
+        (up_high, up_low), (down_high, down_low) = (two_parts(v) for v in pieces[c])
+        up_high, up_low, down_high, down_low = (v.astype(F32) for v in (up_high, up_low, down_high, down_low))
+        up = jnp.where(lane == 47, up_low, jnp.where((lane == 15) | (lane == 31), up_high, 0.0))
+        down = jnp.where(lane == 32, down_low, jnp.where((lane == 0) | (lane == 16), down_high, 0.0))
+        field_ref[here, 3 * height : 3 * height + LANES] = (up + down).astype(BF16)
+
+
+GROUP = 8
+STEP = 4
+SIDE = 4
+
+
+def weight_rows(data, cell, sub16, height):
+    node_a = jnp.where(cell >= 0, cell >> 7, 2 * height)
+    below, same, above = quad_weights(data)
+    parts = [two_parts(w[0:1, :]) for w in (below, same, above)]
+
+    def wide(v):
+        return jnp.broadcast_to(v, (16, CAP))
+
+    def wide16(v):
+        return wide(v.astype(F32).astype(BF16))
+
+    a_in, a_page = node_a & 15, node_a >> 4
+    a_next = jnp.where(a_in == 15, a_page + 1, jnp.where(a_in == 0, a_page - 1, -9))
+    in16, page16, next16 = wide16(a_in), wide16(a_page), wide16(a_next)
+    is_below, is_same, is_above = sub16 == in16 - BF16(1), sub16 == in16, sub16 == in16 + BF16(1)
+    wrap_up, wrap_down = sub16 == in16 - BF16(15), sub16 == in16 + BF16(15)
+    none = jnp.zeros((16, CAP), BF16)
+    near, far = [], []
+    for h in range(2):
+        low, mid, high = (wide(p[h]) for p in parts)
+        near.append(jnp.where(is_below, low, jnp.where(is_same, mid, jnp.where(is_above, high, none))))
+        far.append(jnp.where(wrap_up, high, jnp.where(wrap_down, low, none)))
+    return near, far, page16, next16, none
+
+
+def build_weights(data, cell, weight_ref, lanes, height):
+    sub16 = lax.broadcasted_iota(I32, (16, CAP), 0).astype(F32).astype(BF16)
+    near, far, page16, next16, none = weight_rows(data, cell, sub16, height)
+    for c in range(height // 16):
+        here_c, next_c = page16 == BF16(c), next16 == BF16(c)
+        for h in range(2):
+            rows = jnp.where(here_c, near[h], jnp.where(next_c, far[h], none))
+            at = h * height + 16 * c
+            weight_ref[at : at + 16, lanes] = rows
+    out_c = (next16 == BF16(-1)) | (next16 == BF16(height // 16))
+    for k, h in enumerate((0, 1, 0)):
+        at = 2 * height + 16 * k
+        weight_ref[at : at + 16, lanes] = jnp.where(out_c, far[h], none)
+
+
+def mix(field_ref, weight_ref, height):
+    weights = weight_ref[...]
+    stacked = jnp.concatenate([weights[0 : 2 * height], weights[0:height], weights[2 * height :]], axis=0)
+    return jnp.dot(field_ref[:, 0 : 3 * height + 48], stacked, preferred_element_type=F32)
+
+
+def pick_columns(data, cell, mixed_ref, lanes, width):
+    sub8 = lax.broadcasted_iota(I32, (8, CAP), 0)
     node_b = cell & 127
-    below, same, above = quad_weights(data[0:1, :])
-    left, mid, right = quad_weights(data[1:2, :])
-    a16 = node_a.astype(F32).astype(BF16)
-    is_same = row_ids == a16
-    is_below = row_ids == a16 - BF16(1)
-    is_above = row_ids == a16 + BF16(1)
-    weights = []
-    for part in zip(two_parts(below), two_parts(same), two_parts(above)):
-        weights.append(
-            jnp.where(is_below, part[0], jnp.where(is_same, part[1], jnp.where(is_above, part[2], BF16(0))))
-        )
-    dot = functools.partial(jnp.dot, preferred_element_type=F32)
-    mixed = dot(high_ref[...], weights[0]) + dot(high_ref[...], weights[1]) + dot(low_ref[...], weights[0])
-    first = node_a == 0
-    edge = jnp.where(first, below, jnp.where(node_a == height - 1, above, 0.0))
-    up = jnp.concatenate([up_ref[...]] * 2, axis=1)
-    down = jnp.concatenate([down_ref[...]] * 2, axis=1)
-    mixed = mixed + jnp.where(first, up, down) * edge
-    cols = jnp.where(
-        col_ids == node_b - 1, left, jnp.where(col_ids == node_b, mid, jnp.where(col_ids == node_b + 1, right, 0.0))
-    )
-    at_left = jnp.where(node_b == 0, left, 0.0)
-    at_right = jnp.where(node_b == width - 1, right, 0.0)
+    trio = quad_weights(data)
+
+    def wide(v):
+        return jnp.broadcast_to(v, (8, CAP))
+
+    low, mid, high = (wide(w[1:2, :]) for w in trio)
+    b_in, b_page = wide(node_b & 7), wide(node_b >> 3)
+    b_next = jnp.where(b_in == 7, b_page + 1, jnp.where(b_in == 0, b_page - 1, -9))
+    near = jnp.where(sub8 == b_in - 1, low, jnp.where(sub8 == b_in, mid, jnp.where(sub8 == b_in + 1, high, 0.0)))
+    far = jnp.where(sub8 == b_in - 7, high, jnp.where(sub8 == b_in + 7, low, 0.0))
+    picked = [[jnp.zeros((8, CAP), F32)] * 2 for _ in range(2)]
+    for c in range(width // 8):
+        here_c, next_c = b_page == c, b_next == c
+        for k in range(2):
+            at = k * width + 8 * c
+            block = mixed_ref[at : at + 8, lanes]
+            picked[k][0] = jnp.where(here_c, block, picked[k][0])
+            picked[k][1] = jnp.where(next_c, block, picked[k][1])
     speed = []
-    for c in range(2):
-        inner = jnp.sum(mixed[c * width : (c + 1) * width, :] * cols, axis=0, keepdims=True)
-        side = 2 * width + 2 * c
-        speed.append(
-            inner + mixed[side : side + 1, :] * at_left + mixed[side + 1 : side + 2, :] * at_right
-        )
-    shift = jnp.where(sub_ids == 2, speed[0], jnp.where(sub_ids == 3, speed[1], 0.0))
-    out_ref[:, here] = data + step_length * shift
-
-
-GROUP = 8
+    for k in range(2):
+        side = 2 * width + 2 * k
+        other = jnp.where(b_next == -1, wide(mixed_ref[side : side + 1, lanes]), picked[k][1])
+        other = jnp.where(b_next == width // 8, wide(mixed_ref[side + 1 : side + 2, lanes]), other)
+        speed.append(jnp.sum(picked[k][0] * near + other * far, axis=0, keepdims=True))
+    shift = jnp.where(sub8 == 2, speed[0], jnp.where(sub8 == 3, speed[1], 0.0))
+    return data + step_length * shift
+
+
+def build_step(base, arrived_ref, cell_ref, weight_ref, height):
+    for i in range(STEP):
+        s = base + i
+        here = pl.ds(pl.multiple_of(s * CAP, CAP), CAP)
+        lanes = slice(i * CAP, (i + 1) * CAP)
+        build_weights(arrived_ref[:, here], cell_ref[s], weight_ref, lanes, height)
+
+
+def pick_step(base, arrived_ref, cell_ref, out_ref, mixed_ref, width):
+    for i in range(STEP):
+        s = base + i
+        here = pl.ds(pl.multiple_of(s * CAP, CAP), CAP)
+        lanes = slice(i * CAP, (i + 1) * CAP)
+        out_ref[:, here] = pick_columns(arrived_ref[:, here], cell_ref[s], mixed_ref, lanes, width)
+
+
+def wrapped(at, step, length):
+    to = at + step
+    return jnp.where(to >= length, to - length, to)
 
 
 def rebin_kernel(
     sizes, part_ref, key_ref, a_ref, b_ref, vel_ref, out_ref, cell_ref,
     pos_ref, acc_ref, sorted_ref, sorted_cell_ref, table_ref, table_smem,
-    send_ref, send_cell_ref, turned_ref, rows_ref, cols_ref, high_ref, low_ref, up_ref, down_ref,
+    send_ref, send_cell_ref, turned_ref, rows_ref, cols_ref, field_ref, arrived_ref,
+    weight0_ref, weight1_ref, mixed0_ref, mixed1_ref,
     table_sem, send_sem, send_cell_sem, recv_sem, recv_cell_sem, halo_send, halo_recv,
 ):
     nx, ny, nz = sizes
     total = nx * ny * nz
-    side = 4
     x, y, z = (lax.axis_index(a) for a in AXES)
     me = (x * ny + y) * nz + z
     tiles = ny * nz
     tile = y * nz + z
     height, width = vel_ref.shape[1], vel_ref.shape[2]
-
-    def peer(k, sign):
-        dx = lax.rem(k // tiles + nx // 2, nx)
-        dy = lax.rem(k // (side * nz) + ny // side // 2, ny // side)
-        dyx = lax.rem(k // nz + side // 2, side)
-        dz = lax.rem(k, nz)
-        if sign < 0:
-            dx, dy, dyx, dz = nx - dx, ny // side - dy, side - dyx, nz - dz
-        to_x = lax.rem(x + dx, nx)
-        to_y = lax.rem(y // side + dy, ny // side) * side + lax.rem(lax.rem(y, side) + dyx, side)
-        to_z = lax.rem(z + dz, nz)
-        return (to_x * ny + to_y) * nz + to_z, (to_x, to_y, to_z)
-
-    own = ((nx // 2) * (ny // side) + ny // side // 2) * side * nz + (side // 2) * nz
+    outer, inner = y // SIDE, y % SIDE
+    steps = [(a, b) for a in (2, 3, 0, 1) for b in (2, 3, 0, 1)]
+    ahead_x = [wrapped(x, d, nx) for d in range(nx)]
+    ahead_y = [wrapped(outer, d, ny // SIDE) for d in range(ny // SIDE)]
+    ahead_i = [wrapped(inner, d, SIDE) for d in range(SIDE)]
+    ahead_z = [z, 1 - z]
 
     barrier = pltpu.get_barrier_semaphore()
-
-    def greet(k, carry):
-        @pl.when(k != own)
-        def tell():
-            pl.semaphore_signal(barrier, inc=1, device_id=peer(k, 1)[1], device_id_type=MESH)
-        return carry
-
-    lax.fori_loop(0, total, greet, 0)
+    for a, b in steps:
+        for i in range(SIDE):
+            for c in range(nz):
+                if (a, b, i, c) != (0, 0, 0, 0):
+                    device = (ahead_x[a], ahead_y[b] * SIDE + ahead_i[i], ahead_z[c])
+                    pl.semaphore_signal(barrier, inc=1, device_id=device, device_id_type=MESH)
     turned_ref[0] = vel_ref[0].T
     turned_ref[1] = vel_ref[1].T
 
     halos = []
-    for i, dx in enumerate((1, -1)):
-        to_x = lax.rem(x + dx + nx, nx)
+    for i, dx in enumerate((1, nx - 1)):
         edge = vel_ref.at[:, pl.ds(height - 8 if dx == 1 else 0, 8), :]
-        for j, dt in enumerate((1, 0, -1)):
-            halos.append((edge, rows_ref.at[3 * i + j], to_x, lax.rem(tile + dt + tiles, tiles)))
-    for i, dt in enumerate((1, -1)):
+        for j, dt in enumerate((1, 0, tiles - 1)):
+            halos.append((edge, rows_ref.at[3 * i + j], ahead_x[dx], wrapped(tile, dt, tiles)))
+    for i, dt in enumerate((1, tiles - 1)):
         edge = turned_ref.at[:, pl.ds(width - 8 if dt == 1 else 0, 8), :]
-        halos.append((edge, cols_ref.at[i], x, lax.rem(tile + dt + tiles, tiles)))
+        halos.append((edge, cols_ref.at[i], x, wrapped(tile, dt, tiles)))
     halo_copies = [
         pltpu.make_async_remote_copy(
             src_ref=src, dst_ref=dst, send_sem=halo_send.at[k], recv_sem=halo_recv.at[k],
-            device_id=(to_x, to_t // nz, lax.rem(to_t, nz)), device_id_type=MESH,
+            device_id=(to_x, to_t // nz, to_t % nz), device_id_type=MESH,
         )
         for k, (src, dst, to_x, to_t) in enumerate(halos)
     ]
@@ -273,15 +328,21 @@
 
     mine = pl.ds(pl.multiple_of(me * CAP, CAP), CAP)
 
+    def first_of(a, b):
+        return (ahead_x[a] * (ny // SIDE) + ahead_y[b]) * GROUP
+
     def send_group(g):
-        def send(i, carry):
-            k = g * GROUP + i
-            there, device = peer(k, 1)
-
-            @pl.when(k != own)
-            def remote():
+        a, b = steps[g]
+        for i in range(SIDE):
+            for c in range(nz):
+                there = first_of(a, b) + ahead_i[i] * nz + ahead_z[c]
+                if (a, b, i, c) == (0, 0, 0, 0):
+                    pltpu.make_async_copy(send_ref.at[there], arrived_ref.at[:, mine], recv_sem.at[g]).start()
+                    pltpu.make_async_copy(send_cell_ref.at[there], cell_ref.at[me], recv_cell_sem.at[g]).start()
+                    continue
+                device = (ahead_x[a], ahead_y[b] * SIDE + ahead_i[i], ahead_z[c])
                 pltpu.make_async_remote_copy(
-                    src_ref=send_ref.at[there], dst_ref=out_ref.at[:, mine], send_sem=send_sem,
+                    src_ref=send_ref.at[there], dst_ref=arrived_ref.at[:, mine], send_sem=send_sem,
                     recv_sem=recv_sem.at[g], device_id=device, device_id_type=MESH,
                 ).start()
                 pltpu.make_async_remote_copy(
@@ -289,49 +350,57 @@
                     recv_sem=recv_cell_sem.at[g], device_id=device, device_id_type=MESH,
                 ).start()
 
-            @pl.when(k == own)
-            def local():
-                pltpu.make_async_copy(send_ref.at[there], out_ref.at[:, mine], recv_sem.at[g]).start()
-                pltpu.make_async_copy(send_cell_ref.at[there], cell_ref.at[me], recv_cell_sem.at[g]).start()
-
+    for g, (a, b) in enumerate(steps):
+        base = first_of(a, b)
+
+        def expand_one(i, carry, base=base):
+            expand(base + i, sorted_ref, sorted_cell_ref, table_smem, send_ref, send_cell_ref)
             return carry
 
-        lax.fori_loop(0, GROUP, send, 0)
-
-    def expand_group(g, carry):
-        for i in range(GROUP):
-            there = peer(g * GROUP + i, 1)[0]
-            expand(there, sorted_ref, sorted_cell_ref, table_smem, send_ref, send_cell_ref)
-
-        @pl.when(g > 0)
-        def before():
+        lax.fori_loop(0, GROUP, expand_one, 0, unroll=True)
+        if g > 0:
             send_group(g - 1)
-
-        return carry
-
-    groups = total // GROUP
-    lax.fori_loop(0, groups, expand_group, 0)
+    groups = len(steps)
     send_group(groups - 1)
 
     for c in halo_copies:
         c.wait()
-    prepare_field(sizes, turned_ref, rows_ref, cols_ref, high_ref, low_ref, up_ref, down_ref)
-
-    def finish_group(g, carry):
-        blocks = out_ref.at[:, pl.ds(0, GROUP * CAP)]
+    prepare_field(sizes, turned_ref, rows_ref, cols_ref, field_ref)
+
+    def source_base(g):
+        back_x = (x + 2 * nx - 2 - g // 4) % nx
+        back_y = (outer + 2 * (ny // SIDE) - 2 - g % 4) % (ny // SIDE)
+        return (back_x * (ny // SIDE) + back_y) * GROUP
+
+    def arrive(g):
+        blocks = arrived_ref.at[:, pl.ds(0, GROUP * CAP)]
         pltpu.make_async_copy(blocks, blocks, recv_sem.at[g]).wait()
         few = cell_ref.at[pl.ds(0, GROUP)]
         pltpu.make_async_copy(few, few, recv_cell_sem.at[g]).wait()
 
-        def one(i, inner):
-            source = peer(g * GROUP + i, -1)[0]
-            interpolate_source(source, out_ref, cell_ref, high_ref, low_ref, up_ref, down_ref)
-            return inner
-
-        lax.fori_loop(0, GROUP, one, 0, unroll=2)
-        return carry
-
-    lax.fori_loop(0, groups, finish_group, 0)
+    build = lambda base, ref: build_step(base, arrived_ref, cell_ref, ref, height)
+    pick = lambda base, ref: pick_step(base, arrived_ref, cell_ref, out_ref, ref, width)
+    arrive(0)
+    start = source_base(0)
+    build(start, weight0_ref)
+    mixed0_ref[...] = mix(field_ref, weight0_ref, height)
+    build(start + STEP, weight1_ref)
+
+    def one_group(g, before):
+        arrive(g)
+        base = source_base(g)
+        mixed1_ref[...] = mix(field_ref, weight1_ref, height)
+        pick(before, mixed0_ref)
+        build(base, weight0_ref)
+        mixed0_ref[...] = mix(field_ref, weight0_ref, height)
+        pick(before + STEP, mixed1_ref)
+        build(base + STEP, weight1_ref)
+        return base
+
+    last = lax.fori_loop(1, groups, one_group, start)
+    mixed1_ref[...] = mix(field_ref, weight1_ref, height)
+    pick(last, mixed0_ref)
+    pick(last + STEP, mixed1_ref)
     some = send_ref.at[pl.ds(0, total - 1)]
     some_cell = send_cell_ref.at[pl.ds(0, total - 1)]
     pltpu.make_async_copy(some, some, send_sem).wait()
@@ -365,10 +434,12 @@
             pltpu.VMEM((parts, width, height), F32),
             pltpu.VMEM((6, parts, 8, width), F32),
             pltpu.VMEM((2, parts, 8, height), F32),
-            pltpu.VMEM((2 * width + 8, height), BF16),
-            pltpu.VMEM((2 * width + 8, height), BF16),
-            pltpu.VMEM((2 * width + 8, LANES), F32),
-            pltpu.VMEM((2 * width + 8, LANES), F32),
+            pltpu.VMEM((2 * width + 8, 3 * height + LANES), BF16),
+            pltpu.VMEM((8, owners * CAP), F32),
+            pltpu.VMEM((2 * height + 48, STEP * CAP), BF16),
+            pltpu.VMEM((2 * height + 48, STEP * CAP), BF16),
+            pltpu.VMEM((2 * width + 8, STEP * CAP), F32),
+            pltpu.VMEM((2 * width + 8, STEP * CAP), F32),
             dma, dma, dma, dma((groups,)), dma((groups,)), dma((8,)), dma((8,)),
         ],
         compiler_params=pltpu.CompilerParams(collective_id=0, has_side_effects=True),

time: 94.1 us -> 60 us (0.64)
  the two profiles are of different devices: /device:TPU:47 before, /device:TPU:25 now
where the time goes in v3:
time: 60 us; the launch traced here: 59.8 us
  Pallas kernels  56.2 us (94%)
  local copies, waits for them, and re-layouts  2.97 us (5%)
  between operations  0.65 us (1%)
    pallas_call x1, Pallas kernels, shards(): pl.pallas_call(functools.partial(rebin_kernel, sizes), out_shape=(jax.Sha...  56.2 us
    unnamed x4, local copies, waits for them, and re-layouts  2.97 us

profile of v3, /device:TPU:25, one launch (start us, length us, event | category | flops | bytes accessed | tf_op | source)
XLA Modules:
  0.0 59.8 jit_solution(4132505962294265471)
XLA Ops:
  0.6 56.2 %rebin.1 = (f32[8,32768]{1,0:T(8,128)}, s32[128,1,256]{2,1,0:T(1,128)}) custom-call(f32[8,8192]{1,0:T(8,128)} %part_ref.1, s32[1,8192]{1,0:T(1,128)} %bitcast.5, s32[1,8192]{1,0:T(1,128)} %bitcast.6, s32[1,8192]{1,0:T(1,128)} %bitcast.7, f32[2,256,128]{2,1,0:T(8,128)} %vel_ref.1), custom_call_target="tpu_custom_call" | custom-call | tf_op jit(solution)/shard_map/rebin/pallas_call | solution.py:417
  56.8 0.0 copy-start
  56.8 2.3 %copy.9 = f32[8,32768]{1,0:T(8,128)} copy(f32[8,32768]{1,0:T(8,128)} %get-tuple-element.8) | data formatting | bytes 2097152
  59.1 0.0 copy-done
  59.1 0.7 %copy.10 = s32[32768]{0:T(1024)} copy(s32[32768]{0:T(1024)S(1)} %bitcast.4) | data formatting | bytes 262144
Async XLA Ops:
  56.8 2.3 %copy-start = (s32[128,1,256]{2,1,0:T(1,128)S(1)}, s32[128,1,256]{2,1,0:T(1,128)}, u32[]{:S(2)}) copy-start(s32[128,1,256]{2,1,0:T(1,128)} %get-tuple-element.5) | copy-start | bytes 393220

commit v4 on v3

--- a/solution.py
+++ b/solution.py
@@ -11,7 +11,7 @@
 MESH = pl.DeviceIdType.MESH
 F32, BF16, I32 = jnp.float32, jnp.bfloat16, jnp.int32
 CAP = 256
-CHUNK = 1024
+CHUNK = 2048
 LANES = 128
 step_length = 0.5
 
@@ -41,7 +41,7 @@
             total = total + hot[:, j * LANES : (j + 1) * LANES]
         return total
 
-    spread = lax.fori_loop(0, chunks, count_chunk, jnp.zeros((owners, LANES), F32))
+    spread = lax.fori_loop(0, chunks, count_chunk, jnp.zeros((owners, LANES), F32), unroll=True)
     hist = jnp.broadcast_to(jnp.sum(spread, axis=1, keepdims=True), (owners, owners))
     row = lax.broadcasted_iota(I32, (owners, owners), 0)
     col = lax.broadcasted_iota(I32, (owners, owners), 1)
@@ -67,7 +67,7 @@
             base = base + upto[:, CAP - 1 : CAP]
         return base
 
-    lax.fori_loop(0, chunks, rank_chunk, starts[:, 0:1])
+    lax.fori_loop(0, chunks, rank_chunk, starts[:, 0:1], unroll=True)
     between()
 
     acc_ref[...] = jnp.zeros_like(acc_ref)
@@ -92,7 +92,7 @@
         )
         return carry
 
-    lax.fori_loop(0, chunks, place_chunk, 0)
+    lax.fori_loop(0, chunks, place_chunk, 0, unroll=True)
 
     cells = (acc_ref[512:544, :] * 128.0 + acc_ref[544:576, :]).astype(I32)
     for h in range(32):
@@ -125,7 +125,7 @@
         send_cell_ref[d, :, here] = jnp.where(lanes1 < live - j * LANES, cell, -1)
 
 
-def prepare_field(sizes, turned_ref, rows_ref, cols_ref, field_ref):
+def prepare_field(sizes, turned_ref, rows_ref, cols_ref, field_ref, up_ref, down_ref):
     nx, ny, nz = sizes
     width, height = turned_ref.shape[1], turned_ref.shape[2]
     x = lax.axis_index("gx")
@@ -142,28 +142,18 @@
         field_ref[here, 0:height] = high
         field_ref[here, height : 2 * height] = high
         field_ref[here, 2 * height : 3 * height] = low
-    lane = lax.broadcasted_iota(I32, (1, LANES), 1)
-    pieces = [[], [], []]
-    for first, row, there in ((0, 7, x > 0), (3, 0, x < nx - 1)):
+    for ref, first, row, there in ((up_ref, 0, 7, x > 0), (down_ref, 3, 0, x < nx - 1)):
+        corner = []
         for c in range(2):
             tile8 = jnp.where(there, rows_ref[first + 1, c], 0.0)
-            pieces[c].append(jnp.broadcast_to(tile8.T[:, row : row + 1], (width, LANES)))
-        corner = []
-        for c in range(2):
+            line = tile8.T[:, row : row + 1]
+            ref[c * width : (c + 1) * width, :] = jnp.broadcast_to(line, (width, LANES))
             from_left = rows_ref[first, c][row : row + 1, width - 1 : width]
             from_right = rows_ref[first + 2, c][row : row + 1, 0:1]
             corner.append(jnp.where(there & has_left, from_left, 0.0))
             corner.append(jnp.where(there & has_right, from_right, 0.0))
         corner = jnp.concatenate(corner + [jnp.zeros((4, 1), F32)], axis=0)
-        pieces[2].append(jnp.broadcast_to(corner, (8, LANES)))
-    for c in range(3):
-        rows = pieces[c][0].shape[0]
-        here = slice(c * width, c * width + rows)
-        (up_high, up_low), (down_high, down_low) = (two_parts(v) for v in pieces[c])
-        up_high, up_low, down_high, down_low = (v.astype(F32) for v in (up_high, up_low, down_high, down_low))
-        up = jnp.where(lane == 47, up_low, jnp.where((lane == 15) | (lane == 31), up_high, 0.0))
-        down = jnp.where(lane == 32, down_low, jnp.where((lane == 0) | (lane == 16), down_high, 0.0))
-        field_ref[here, 3 * height : 3 * height + LANES] = (up + down).astype(BF16)
+        ref[2 * width :, :] = jnp.broadcast_to(corner, (8, LANES))
 
 
 GROUP = 8
@@ -205,19 +195,15 @@
             rows = jnp.where(here_c, near[h], jnp.where(next_c, far[h], none))
             at = h * height + 16 * c
             weight_ref[at : at + 16, lanes] = rows
-    out_c = (next16 == BF16(-1)) | (next16 == BF16(height // 16))
-    for k, h in enumerate((0, 1, 0)):
-        at = 2 * height + 16 * k
-        weight_ref[at : at + 16, lanes] = jnp.where(out_c, far[h], none)
 
 
 def mix(field_ref, weight_ref, height):
     weights = weight_ref[...]
-    stacked = jnp.concatenate([weights[0 : 2 * height], weights[0:height], weights[2 * height :]], axis=0)
-    return jnp.dot(field_ref[:, 0 : 3 * height + 48], stacked, preferred_element_type=F32)
-
-
-def pick_columns(data, cell, mixed_ref, lanes, width):
+    stacked = jnp.concatenate([weights, weights[0:height]], axis=0)
+    return jnp.dot(field_ref[...], stacked, preferred_element_type=F32)
+
+
+def pick_columns(data, cell, mixed_ref, up_ref, down_ref, lanes, height, width):
     sub8 = lax.broadcasted_iota(I32, (8, CAP), 0)
     node_b = cell & 127
     trio = quad_weights(data)
@@ -230,19 +216,27 @@
     b_next = jnp.where(b_in == 7, b_page + 1, jnp.where(b_in == 0, b_page - 1, -9))
     near = jnp.where(sub8 == b_in - 1, low, jnp.where(sub8 == b_in, mid, jnp.where(sub8 == b_in + 1, high, 0.0)))
     far = jnp.where(sub8 == b_in - 7, high, jnp.where(sub8 == b_in + 7, low, 0.0))
+    first = cell < width
+    edge = jnp.where(first, trio[0][0:1, :], jnp.where(cell >= (height - 1) * width, trio[2][0:1, :], 0.0))
+    edge, first = wide(jnp.where(cell >= 0, edge, 0.0)), wide(cell) < width
+
+    def rows_at(at):
+        up = jnp.concatenate([up_ref[at : at + 8, :]] * 2, axis=1)
+        down = jnp.concatenate([down_ref[at : at + 8, :]] * 2, axis=1)
+        return mixed_ref[at : at + 8, lanes] + jnp.where(first, up, down) * edge
+
     picked = [[jnp.zeros((8, CAP), F32)] * 2 for _ in range(2)]
     for c in range(width // 8):
         here_c, next_c = b_page == c, b_next == c
         for k in range(2):
-            at = k * width + 8 * c
-            block = mixed_ref[at : at + 8, lanes]
+            block = rows_at(k * width + 8 * c)
             picked[k][0] = jnp.where(here_c, block, picked[k][0])
             picked[k][1] = jnp.where(next_c, block, picked[k][1])
     speed = []
+    sides = rows_at(2 * width)
     for k in range(2):
-        side = 2 * width + 2 * k
-        other = jnp.where(b_next == -1, wide(mixed_ref[side : side + 1, lanes]), picked[k][1])
-        other = jnp.where(b_next == width // 8, wide(mixed_ref[side + 1 : side + 2, lanes]), other)
+        other = jnp.where(b_next == -1, wide(sides[2 * k : 2 * k + 1, :]), picked[k][1])
+        other = jnp.where(b_next == width // 8, wide(sides[2 * k + 1 : 2 * k + 2, :]), other)
         speed.append(jnp.sum(picked[k][0] * near + other * far, axis=0, keepdims=True))
     shift = jnp.where(sub8 == 2, speed[0], jnp.where(sub8 == 3, speed[1], 0.0))
     return data + step_length * shift
@@ -256,12 +250,14 @@
         build_weights(arrived_ref[:, here], cell_ref[s], weight_ref, lanes, height)
 
 
-def pick_step(base, arrived_ref, cell_ref, out_ref, mixed_ref, width):
+def pick_step(base, arrived_ref, cell_ref, out_ref, mixed_ref, up_ref, down_ref, height, width):
     for i in range(STEP):
         s = base + i
         here = pl.ds(pl.multiple_of(s * CAP, CAP), CAP)
         lanes = slice(i * CAP, (i + 1) * CAP)
-        out_ref[:, here] = pick_columns(arrived_ref[:, here], cell_ref[s], mixed_ref, lanes, width)
+        out_ref[:, here] = pick_columns(
+            arrived_ref[:, here], cell_ref[s], mixed_ref, up_ref, down_ref, lanes, height, width
+        )
 
 
 def wrapped(at, step, length):
@@ -270,21 +266,26 @@
 
 
 def rebin_kernel(
-    sizes, part_ref, key_ref, a_ref, b_ref, vel_ref, out_ref, cell_ref,
+    sizes, part_in, key_in, a_in, b_in, vel_in, out_ref, cell_ref,
+    part_ref, key_ref, a_ref, b_ref, vel_ref,
     pos_ref, acc_ref, sorted_ref, sorted_cell_ref, table_ref, table_smem,
-    send_ref, send_cell_ref, turned_ref, rows_ref, cols_ref, field_ref, arrived_ref,
+    send_ref, send_cell_ref, turned_ref, rows_ref, cols_ref, field_ref, up_ref, down_ref, arrived_ref,
     weight0_ref, weight1_ref, mixed0_ref, mixed1_ref,
-    table_sem, send_sem, send_cell_sem, recv_sem, recv_cell_sem, halo_send, halo_recv,
+    load_sem, table_sem, send_sem, send_cell_sem, recv_sem, recv_cell_sem, halo_send, halo_recv,
 ):
     nx, ny, nz = sizes
     total = nx * ny * nz
+    pairs = ((key_in, key_ref), (vel_in, vel_ref), (part_in, part_ref), (a_in, a_ref), (b_in, b_ref))
+    loads = [pltpu.make_async_copy(src, dst, load_sem.at[k]) for k, (src, dst) in enumerate(pairs)]
+    for load in loads:
+        load.start()
     x, y, z = (lax.axis_index(a) for a in AXES)
     me = (x * ny + y) * nz + z
     tiles = ny * nz
     tile = y * nz + z
     height, width = vel_ref.shape[1], vel_ref.shape[2]
     outer, inner = y // SIDE, y % SIDE
-    steps = [(a, b) for a in (2, 3, 0, 1) for b in (2, 3, 0, 1)]
+    steps = [(0, 0), (0, 1), (1, 0), (0, 3), (3, 0), (1, 1), (3, 3), (1, 3), (3, 1), (0, 2), (2, 0), (1, 2), (2, 1), (3, 2), (2, 3), (2, 2)]
     ahead_x = [wrapped(x, d, nx) for d in range(nx)]
     ahead_y = [wrapped(outer, d, ny // SIDE) for d in range(ny // SIDE)]
     ahead_i = [wrapped(inner, d, SIDE) for d in range(SIDE)]
@@ -297,8 +298,6 @@
                 if (a, b, i, c) != (0, 0, 0, 0):
                     device = (ahead_x[a], ahead_y[b] * SIDE + ahead_i[i], ahead_z[c])
                     pl.semaphore_signal(barrier, inc=1, device_id=device, device_id_type=MESH)
-    turned_ref[0] = vel_ref[0].T
-    turned_ref[1] = vel_ref[1].T
 
     halos = []
     for i, dx in enumerate((1, nx - 1)):
@@ -317,10 +316,16 @@
     ]
 
     def between():
+        loads[1].wait()
+        turned_ref[0] = vel_ref[0].T
+        turned_ref[1] = vel_ref[1].T
         pl.semaphore_wait(barrier, total - 1)
         for c in halo_copies:
             c.start()
-
+        for load in loads[2:]:
+            load.wait()
+
+    loads[0].wait()
     sort_phase(
         part_ref, key_ref, a_ref, b_ref, pos_ref, acc_ref, sorted_ref, sorted_cell_ref,
         table_ref, table_smem, table_sem, total, between,
@@ -365,11 +370,14 @@
 
     for c in halo_copies:
         c.wait()
-    prepare_field(sizes, turned_ref, rows_ref, cols_ref, field_ref)
+    prepare_field(sizes, turned_ref, rows_ref, cols_ref, field_ref, up_ref, down_ref)
 
     def source_base(g):
-        back_x = (x + 2 * nx - 2 - g // 4) % nx
-        back_y = (outer + 2 * (ny // SIDE) - 2 - g % 4) % (ny // SIDE)
+        shift = jnp.int32(2) * g
+        step_x = lax.shift_right_arithmetic(jnp.int32(-1369213168), shift) & 3
+        step_y = lax.shift_right_arithmetic(jnp.int32(-1182141244), shift) & 3
+        back_x = (x + nx - step_x) % nx
+        back_y = (outer + ny // SIDE - step_y) % (ny // SIDE)
         return (back_x * (ny // SIDE) + back_y) * GROUP
 
     def arrive(g):
@@ -379,7 +387,9 @@
         pltpu.make_async_copy(few, few, recv_cell_sem.at[g]).wait()
 
     build = lambda base, ref: build_step(base, arrived_ref, cell_ref, ref, height)
-    pick = lambda base, ref: pick_step(base, arrived_ref, cell_ref, out_ref, ref, width)
+    pick = lambda base, ref: pick_step(
+        base, arrived_ref, cell_ref, out_ref, ref, up_ref, down_ref, height, width
+    )
     arrive(0)
     start = source_base(0)
     build(start, weight0_ref)
@@ -420,9 +430,14 @@
             jax.ShapeDtypeStruct((8, owners * CAP), F32),
             jax.ShapeDtypeStruct((owners, 1, CAP), I32),
         ),
-        in_specs=[vmem] * 5,
+        in_specs=[pl.BlockSpec(memory_space=pltpu.HBM)] * 5,
         out_specs=(vmem,) * 2,
         scratch_shapes=[
+            pltpu.VMEM(particles.shape, F32),
+            pltpu.VMEM((1, count), I32),
+            pltpu.VMEM((1, count), I32),
+            pltpu.VMEM((1, count), I32),
+            pltpu.VMEM(velocity.shape, F32),
             pltpu.VMEM((1, count), I32),
             pltpu.VMEM((576, CAP), F32),
             pltpu.VMEM((67, 8, LANES), F32),
@@ -434,13 +449,15 @@
             pltpu.VMEM((parts, width, height), F32),
             pltpu.VMEM((6, parts, 8, width), F32),
             pltpu.VMEM((2, parts, 8, height), F32),
-            pltpu.VMEM((2 * width + 8, 3 * height + LANES), BF16),
+            pltpu.VMEM((2 * width + 8, 3 * height), BF16),
+            pltpu.VMEM((2 * width + 8, LANES), F32),
+            pltpu.VMEM((2 * width + 8, LANES), F32),
             pltpu.VMEM((8, owners * CAP), F32),
-            pltpu.VMEM((2 * height + 48, STEP * CAP), BF16),
-            pltpu.VMEM((2 * height + 48, STEP * CAP), BF16),
+            pltpu.VMEM((2 * height, STEP * CAP), BF16),
+            pltpu.VMEM((2 * height, STEP * CAP), BF16),
             pltpu.VMEM((2 * width + 8, STEP * CAP), F32),
             pltpu.VMEM((2 * width + 8, STEP * CAP), F32),
-            dma, dma, dma, dma((groups,)), dma((groups,)), dma((8,)), dma((8,)),
+            dma((5,)), dma, dma, dma, dma((groups,)), dma((groups,)), dma((8,)), dma((8,)),
         ],
         compiler_params=pltpu.CompilerParams(collective_id=0, has_side_effects=True),
         name="rebin",

time: 60 us -> 45.6 us (0.76)
  the two profiles are of different devices: /device:TPU:25 before, /device:TPU:1 now
where the time goes in v4:
time: 45.6 us; the launch traced here: 45.4 us
  Pallas kernels  41.8 us (92%)
  local copies, waits for them, and re-layouts  2.97 us (7%)
  between operations  0.65 us (1%)
    pallas_call x1, Pallas kernels, shards(): pl.pallas_call(functools.partial(rebin_kernel, sizes), out_shape=(jax.Sha...  41.8 us
    unnamed x4, local copies, waits for them, and re-layouts  2.97 us

profile of v4, /device:TPU:1, one launch (start us, length us, event | category | flops | bytes accessed | tf_op | source)
XLA Modules:
  0.0 45.4 jit_solution(16807526538998247556)
XLA Ops:
  0.6 41.8 %rebin.1 = (f32[8,32768]{1,0:T(8,128)}, s32[128,1,256]{2,1,0:T(1,128)}) custom-call(f32[8,8192]{1,0:T(8,128)} %part_in.1, s32[1,8192]{1,0:T(1,128)} %bitcast.5, s32[1,8192]{1,0:T(1,128)} %bitcast.6, s32[1,8192]{1,0:T(1,128)} %bitcast.7, f32[2,256,128]{2,1,0:T(8,128)} %vel_in.1), custom_call_target="tpu_custom_call" | custom-call | tf_op jit(solution)/shard_map/rebin/pallas_call | solution.py:427
  42.4 0.0 copy-start
  42.4 2.3 %copy.9 = f32[8,32768]{1,0:T(8,128)} copy(f32[8,32768]{1,0:T(8,128)} %get-tuple-element.8) | data formatting | bytes 2097152
  44.7 0.0 copy-done
  44.7 0.7 %copy.10 = s32[32768]{0:T(1024)} copy(s32[32768]{0:T(1024)S(1)} %bitcast.4) | data formatting | bytes 262144
Async XLA Ops:
  42.4 2.3 %copy-start = (s32[128,1,256]{2,1,0:T(1,128)S(1)}, s32[128,1,256]{2,1,0:T(1,128)}, u32[]{:S(2)}) copy-start(s32[128,1,256]{2,1,0:T(1,128)} %get-tuple-element.5) | copy-start | bytes 393220

commit v5 on v4

--- a/solution.py
+++ b/solution.py
@@ -427,8 +427,8 @@
     binned, binned_cell = pl.pallas_call(
         functools.partial(rebin_kernel, sizes),
         out_shape=(
-            jax.ShapeDtypeStruct((8, owners * CAP), F32),
-            jax.ShapeDtypeStruct((owners, 1, CAP), I32),
+            pltpu.VMEM((8, owners * CAP), F32),
+            pltpu.VMEM((owners, 1, CAP), I32),
         ),
         in_specs=[pl.BlockSpec(memory_space=pltpu.HBM)] * 5,
         out_specs=(vmem,) * 2,

time: 45.6 us -> 43.1 us (0.945)
  local copies, waits for them, and re-layouts: 2.97 us -> 1.64 us
  Pallas kernels: 41.8 us -> 40.7 us
    unnamed x4 -> x2, local copies, waits for them, and re-layouts: 2.97 us -> 1.64 us
    pallas_call x1, Pallas kernels: 41.8 us -> 40.7 us  [shards(): pl.pallas_call(functools.partial(rebin_kernel, sizes), out_shape=(pltpu.V...]
where the time goes in v5:
time: 43.1 us; the launch traced here: 43 us
  Pallas kernels  40.7 us (94%)
  local copies, waits for them, and re-layouts  1.64 us (4%)
  between operations  0.64 us (1%)
    pallas_call x1, Pallas kernels, shards(): pl.pallas_call(functools.partial(rebin_kernel, sizes), out_shape=(pltpu.V...  40.7 us
    unnamed x2, local copies, waits for them, and re-layouts  1.64 us

profile of v5, /device:TPU:1, one launch (start us, length us, event | category | flops | bytes accessed | tf_op | source)
XLA Modules:
  0.0 43.0 jit_solution(7215183666961963372)
XLA Ops:
  0.6 40.7 %rebin.1 = (f32[8,32768]{1,0:T(8,128)S(1)}, s32[128,1,256]{2,1,0:T(1,128)S(1)}) custom-call(f32[8,8192]{1,0:T(8,128)} %part_in.1, s32[1,8192]{1,0:T(1,128)} %bitcast.5, s32[1,8192]{1,0:T(1,128)} %bitcast.6, s32[1,8192]{1,0:T(1,128)} %bitcast.7, f32[2,256,128]{2,1,0:T(8,128)} %vel_in.1), custom_call_target="tpu_custom_call" | custom-call | tf_op jit(solution)/shard_map/rebin/pallas_call | solution.py:427
  41.4 1.0 %copy.9 = f32[8,32768]{1,0:T(8,128)} copy(f32[8,32768]{1,0:T(8,128)S(1)} %get-tuple-element.6) | data formatting | bytes 2097152
  42.3 0.7 %copy.10 = s32[32768]{0:T(1024)} copy(s32[32768]{0:T(1024)S(1)} %bitcast.4) | data formatting | bytes 262144

commit v6 on v5

--- a/solution.py
+++ b/solution.py
@@ -319,9 +319,6 @@
         loads[1].wait()
         turned_ref[0] = vel_ref[0].T
         turned_ref[1] = vel_ref[1].T
-        pl.semaphore_wait(barrier, total - 1)
-        for c in halo_copies:
-            c.start()
         for load in loads[2:]:
             load.wait()
 
@@ -330,6 +327,9 @@
         part_ref, key_ref, a_ref, b_ref, pos_ref, acc_ref, sorted_ref, sorted_cell_ref,
         table_ref, table_smem, table_sem, total, between,
     )
+    pl.semaphore_wait(barrier, total - 1)
+    for c in halo_copies:
+        c.start()
 
     mine = pl.ds(pl.multiple_of(me * CAP, CAP), CAP)
 

time: 43.1 us -> 42.6 us (0.988)
  Pallas kernels: 40.7 us -> 39.8 us
    pallas_call x1, Pallas kernels: 40.7 us -> 39.8 us  [shards(): pl.pallas_call(functools.partial(rebin_kernel, sizes), out_shape=(pltpu.V...]
where the time goes in v6:
time: 42.6 us; the launch traced here: 42.1 us
  Pallas kernels  39.8 us (93%)
  local copies, waits for them, and re-layouts  1.64 us (4%)
  between operations  0.64 us (2%)
    pallas_call x1, Pallas kernels, shards(): pl.pallas_call(functools.partial(rebin_kernel, sizes), out_shape=(pltpu.V...  39.8 us
    unnamed x2, local copies, waits for them, and re-layouts  1.64 us

profile of v6, /device:TPU:1, one launch (start us, length us, event | category | flops | bytes accessed | tf_op | source)
XLA Modules:
  0.0 42.1 jit_solution(2851899528186389730)
XLA Ops:
  0.6 39.8 %rebin.1 = (f32[8,32768]{1,0:T(8,128)S(1)}, s32[128,1,256]{2,1,0:T(1,128)S(1)}) custom-call(f32[8,8192]{1,0:T(8,128)} %part_in.1, s32[1,8192]{1,0:T(1,128)} %bitcast.5, s32[1,8192]{1,0:T(1,128)} %bitcast.6, s32[1,8192]{1,0:T(1,128)} %bitcast.7, f32[2,256,128]{2,1,0:T(8,128)} %vel_in.1), custom_call_target="tpu_custom_call" | custom-call | tf_op jit(solution)/shard_map/rebin/pallas_call | solution.py:427
  40.5 1.0 %copy.9 = f32[8,32768]{1,0:T(8,128)} copy(f32[8,32768]{1,0:T(8,128)S(1)} %get-tuple-element.6) | data formatting | bytes 2097152
  41.5 0.7 %copy.10 = s32[32768]{0:T(1024)} copy(s32[32768]{0:T(1024)S(1)} %bitcast.4) | data formatting | bytes 262144

commit v7 on v6

--- a/solution.py
+++ b/solution.py
@@ -70,12 +70,11 @@
     lax.fori_loop(0, chunks, rank_chunk, starts[:, 0:1], unroll=True)
     between()
 
-    acc_ref[...] = jnp.zeros_like(acc_ref)
     lane_ids = lax.broadcasted_iota(I32, (CAP, CHUNK), 0)
     page_ids = lax.broadcasted_iota(I32, (32, CHUNK), 0)
 
-    def place_chunk(i, carry):
-        at = pl.ds(pl.multiple_of(i * CHUNK, CHUNK), CHUNK)
+    def place_chunk(i):
+        at = pl.ds(i * CHUNK, CHUNK)
         pos = pos_ref[:, at]
         page = pos >> 8
         lane_hot = (lane_ids == (pos & 255)).astype(F32).astype(BF16)
@@ -86,13 +85,14 @@
         page_hot = (page_ids == page)
         rows.append(jnp.where(page_hot, a_ref[:, at].astype(F32), 0.0).astype(BF16))
         rows.append(jnp.where(page_hot, b_ref[:, at].astype(F32), 0.0).astype(BF16))
-        acc_ref[...] += lax.dot_general(
+        return lax.dot_general(
             jnp.concatenate(rows, axis=0), lane_hot, (((1,), (1,)), ((), ())),
             preferred_element_type=F32,
         )
-        return carry
-
-    lax.fori_loop(0, chunks, place_chunk, 0, unroll=True)
+
+    acc_ref[...] = place_chunk(0)
+    for i in range(1, chunks):
+        acc_ref[...] += place_chunk(i)
 
     cells = (acc_ref[512:544, :] * 128.0 + acc_ref[544:576, :]).astype(I32)
     for h in range(32):

time: 42.6 us -> 42.6 us (level)
  no operation moved by 1% of the time
where the time goes in v7:
time: 42.6 us; the launch traced here: 42.1 us
  Pallas kernels  39.9 us (94%)
  local copies, waits for them, and re-layouts  1.64 us (4%)
  between operations  0.64 us (2%)
    pallas_call x1, Pallas kernels, shards(): pl.pallas_call(functools.partial(rebin_kernel, sizes), out_shape=(pltpu.V...  39.9 us
    unnamed x2, local copies, waits for them, and re-layouts  1.64 us

profile of v7, /device:TPU:1, one launch (start us, length us, event | category | flops | bytes accessed | tf_op | source)
XLA Modules:
  0.0 42.1 jit_solution(2851899528186389730)
XLA Ops:
  0.6 39.9 %rebin.1 = (f32[8,32768]{1,0:T(8,128)S(1)}, s32[128,1,256]{2,1,0:T(1,128)S(1)}) custom-call(f32[8,8192]{1,0:T(8,128)} %part_in.1, s32[1,8192]{1,0:T(1,128)} %bitcast.5, s32[1,8192]{1,0:T(1,128)} %bitcast.6, s32[1,8192]{1,0:T(1,128)} %bitcast.7, f32[2,256,128]{2,1,0:T(8,128)} %vel_in.1), custom_call_target="tpu_custom_call" | custom-call | tf_op jit(solution)/shard_map/rebin/pallas_call | solution.py:427
  40.5 1.0 %copy.9 = f32[8,32768]{1,0:T(8,128)} copy(f32[8,32768]{1,0:T(8,128)S(1)} %get-tuple-element.6) | data formatting | bytes 2097152
  41.5 0.7 %copy.10 = s32[32768]{0:T(1024)} copy(s32[32768]{0:T(1024)S(1)} %bitcast.4) | data formatting | bytes 262144
